TPU v7x, 32 devices: a whole 2x2x4 slice. The times are simulated.
32 devices in a mesh: grp: 4 (over z), pen: 8 (over y, x, core).
Axes of the slice: x: 2, y: 2, z: 4, core: 2. Of those that a mesh axis runs over, the one named last changes fastest.
Arguments:
- cell_offsets: int32 [2, 1048576], P(None, ('grp', 'pen')), may hold values from 0 to 1
- cell_z: int32 [1048576], P(('grp', 'pen')), may hold values from 0 to 255
- frac: float32 [3, 1048576], P(None, ('grp', 'pen')), may hold values from 0 to 1
- charges: float32 [1048576], P(('grp', 'pen')), may hold values from -4 to 4
- tile_counts: int32 [16384], P(('grp', 'pen')), may hold values from 16 to 64, as said below
Outputs:
- forces: float32 [3, 1048576], P(None, ('grp', 'pen'))
- energy: float32 [], replicated
Inputs may be any that keep to these rules, and one draw needn't show every extreme that they name: `tile_counts`: live slots of each tile; some tile holds 64.
All inputs are finite; a program needn't handle non-finite values.
Results may differ from a plain program's by a relative error of at most 0.0003.
Values sent between devices are 32-bit elements; how exact they have to be, the bound alone decides.
No kernel may reach another device: no remote copies, remote signals or barrier semaphores. Data moves between devices by JAX's collectives and lax.ppermute only.
A program may use at most 256 MiB of HBM per device.

v0:
```python
import math

import jax
import jax.numpy as jnp
from jax import lax
from jax.sharding import PartitionSpec as P

KX = 256
KY = 256
KZ = 256
ATOMS = 1048576


ewald_split = 0.6
highest = lax.Precision.HIGHEST


def shifted(block, axis, distance):
    devices = range(lax.axis_size(axis))
    route = [((i - distance) % len(devices), i) for i in devices]
    return lax.ppermute(block, axis, route)


def spline_rows(fracs):
    values = [jnp.ones_like(fracs)]
    fifth = values
    for order in range(2, 7):
        nxt = []
        for j in range(order):
            term = jnp.zeros_like(fracs)
            if j >= 1:
                term = values[j - 1] * (fracs + order - 1 - j)
            if j <= order - 2:
                term = term + values[j] * (1.0 - fracs + j)
            nxt.append(term / (order - 1))
        if order == 5:
            fifth = nxt
        values = nxt
    slopes = []
    for j in range(6):
        term = jnp.zeros_like(fracs)
        if j >= 1:
            term = fifth[j - 1]
        if j <= 4:
            term = term - fifth[j]
        slopes.append(term)
    return (values, slopes)


def tile_weights(offsets, zcell, fracs, charge, counts, size_z):
    slots = charge.shape[-1]
    live = (jnp.arange(slots, dtype=jnp.int32) < counts[..., None]).astype(jnp.float32)
    live_q = charge * live
    theta_x, slope_x = spline_rows(fracs[0])
    theta_y, slope_y = spline_rows(fracs[1])
    theta_z, slope_z = spline_rows(fracs[2])
    footing = jnp.arange(8, dtype=jnp.int32)[:, None]
    cells = jnp.arange(size_z, dtype=jnp.int32)
    weight_x = 0.0
    grade_x = 0.0
    weight_y = 0.0
    grade_y = 0.0
    weight_z = 0.0
    grade_z = 0.0
    for j in range(6):
        hit_x = (footing == offsets[0][..., None, :] + j).astype(jnp.float32)
        hit_y = (footing == offsets[1][..., None, :] + j).astype(jnp.float32)
        hit_z = (cells == (zcell[..., :, None] + j) % size_z).astype(jnp.float32)
        weight_x = weight_x + theta_x[j][..., None, :] * hit_x
        grade_x = grade_x + slope_x[j][..., None, :] * hit_x
        weight_y = weight_y + theta_y[j][..., None, :] * hit_y
        grade_y = grade_y + slope_y[j][..., None, :] * hit_y
        weight_z = weight_z + theta_z[j][..., :, None] * hit_z
        grade_z = grade_z + slope_z[j][..., :, None] * hit_z
    return (weight_x, grade_x, weight_y, grade_y, weight_z, grade_z, live_q)


def modulus(index, length):
    coeffs = (1.0 / 120.0, 26.0 / 120.0, 66.0 / 120.0, 26.0 / 120.0, 1.0 / 120.0)
    real_part = 0.0
    imag_part = 0.0
    for j in range(5):
        angle = (index * j % length).astype(jnp.float32) * (2.0 * math.pi / length)
        real_part = real_part + coeffs[j] * jnp.cos(angle)
        imag_part = imag_part + coeffs[j] * jnp.sin(angle)
    return real_part * real_part + imag_part * imag_part


def influence(index_x, index_y, index_z):
    freq_x = jnp.where(2 * index_x < KX, index_x, index_x - KX).astype(jnp.float32) / KX
    freq_y = jnp.where(2 * index_y < KY, index_y, index_y - KY).astype(jnp.float32) / KY
    freq_z = jnp.where(2 * index_z < KZ, index_z, index_z - KZ).astype(jnp.float32) / KZ
    square = freq_x * freq_x + freq_y * freq_y + freq_z * freq_z
    safe = jnp.where(square > 0, square, 1.0)
    volume = float(KX * KY * KZ)
    value = jnp.exp(-math.pi**2 * safe / ewald_split**2) / (math.pi * volume * safe)
    value = value / (modulus(index_x, KX) * modulus(index_y, KY) * modulus(index_z, KZ))
    return jnp.where(square > 0, value, 0.0)


def dft_tables(length):
    index = jnp.arange(length, dtype=jnp.int32)
    angle = (index[:, None] * index[None, :] % length).astype(jnp.float32) * (
        2.0 * math.pi / length
    )
    return (jnp.cos(angle), jnp.sin(angle))


def z_slots(groups):
    planes = KZ // (2 * groups) + 1
    owner = jnp.arange(groups, dtype=jnp.int32)[:, None]
    within = jnp.arange(planes, dtype=jnp.int32)[None, :]
    ordinary = owner * (planes - 1) + within
    frequency = jnp.where(within < planes - 1, ordinary, jnp.where(owner == 0, KZ // 2, 0))
    plane_weight = jnp.where(
        within < planes - 1, jnp.where(frequency == 0, 1.0, 2.0), jnp.where(owner == 0, 1.0, 0.0)
    )
    frequency = frequency.reshape(-1)
    plane_weight = plane_weight.reshape(-1).astype(jnp.float32)
    position = jnp.arange(KZ, dtype=jnp.int32)
    angle = (frequency[:, None] * position[None, :] % KZ).astype(jnp.float32) * (2.0 * math.pi / KZ)
    usable = (plane_weight > 0).astype(jnp.float32)[:, None]
    return (planes, frequency, plane_weight, jnp.cos(angle) * usable, jnp.sin(angle) * usable)


def forward_complex(data, cos_table, sin_table, shape, axis):
    direct = jnp.dot(cos_table, data, precision=highest).reshape(shape)
    other = jnp.dot(sin_table, data, precision=highest).reshape(shape)
    real_part = jnp.take(direct, 0, axis=axis) + jnp.take(other, 1, axis=axis)
    imag_part = jnp.take(direct, 1, axis=axis) - jnp.take(other, 0, axis=axis)
    return (real_part, imag_part)


def inverse_complex(data, cos_table, sin_table, shape, axis):
    direct = jnp.dot(cos_table, data, precision=highest).reshape(shape)
    other = jnp.dot(sin_table, data, precision=highest).reshape(shape)
    real_part = jnp.take(direct, 0, axis=axis) - jnp.take(other, 1, axis=axis)
    imag_part = jnp.take(other, 0, axis=axis) + jnp.take(direct, 1, axis=axis)
    return (real_part, imag_part)


def spectrum_pen_first(grid, block_x, block_y):
    cos_x, sin_x = dft_tables(KX)
    cos_y, sin_y = dft_tables(KY)
    planes, frequency, plane_weight, cos_z, sin_z = z_slots(lax.axis_size("pen"))
    slot_total = cos_z.shape[0]
    lines = KY // lax.axis_size("grp")
    real_z = jnp.einsum("xyz,kz->ykx", grid, cos_z, precision=highest)
    imag_z = -jnp.einsum("xyz,kz->ykx", grid, sin_z, precision=highest)
    outgoing = jnp.stack([real_z, imag_z], axis=2).reshape(block_y, slot_total * 2 * block_x)
    columns = lax.all_to_all(outgoing, "pen", split_axis=1, concat_axis=0, tiled=True)
    real_y, imag_y = forward_complex(columns, cos_y, sin_y, (KY, planes, 2, block_x), 2)
    sectioned = jnp.transpose(jnp.stack([real_y, imag_y], axis=-1), (2, 0, 1, 3)).reshape(
        block_x, KY * planes * 2
    )
    rows = lax.all_to_all(sectioned, "grp", split_axis=1, concat_axis=0, tiled=True)
    real_x, imag_x = forward_complex(rows, cos_x, sin_x, (KX, lines, planes, 2), 3)
    first = lax.axis_index("pen") * planes
    index_x = jnp.arange(KX, dtype=jnp.int32)[:, None, None]
    index_y = lax.axis_index("grp") * lines + jnp.arange(lines, dtype=jnp.int32)[None, :, None]
    index_z = lax.dynamic_slice_in_dim(frequency, first, planes)[None, None, :]
    local_weight = lax.dynamic_slice_in_dim(plane_weight, first, planes)[None, None, :]
    kernel = influence(index_x, index_y, index_z)
    spectral = 0.5 * jnp.sum(local_weight * kernel * (real_x * real_x + imag_x * imag_x))
    scaled = jnp.stack([kernel * real_x, kernel * imag_x], axis=-1).reshape(KX, lines * planes * 2)
    real_b, imag_b = inverse_complex(scaled, cos_x, sin_x, (KX, lines, planes, 2), 3)
    returning = jnp.stack([real_b, imag_b], axis=-1).reshape(KX, lines * planes * 2)
    rows_home = lax.all_to_all(returning, "grp", split_axis=0, concat_axis=1, tiled=True)
    rows_home = jnp.transpose(rows_home.reshape(block_x, KY, planes, 2), (1, 2, 3, 0)).reshape(
        KY, planes * 2 * block_x
    )
    real_c, imag_c = inverse_complex(rows_home, cos_y, sin_y, (KY, planes, 2, block_x), 2)
    leaving = jnp.stack([real_c, imag_c], axis=2).reshape(KY, planes * 2 * block_x)
    home = lax.all_to_all(leaving, "pen", split_axis=0, concat_axis=1, tiled=True).reshape(
        block_y, slot_total, 2, block_x
    )
    potential = jnp.einsum(
        "ykx,kz->xyz", home[:, :, 0], plane_weight[:, None] * cos_z, precision=highest
    )
    potential = potential - jnp.einsum(
        "ykx,kz->xyz", home[:, :, 1], plane_weight[:, None] * sin_z, precision=highest
    )
    return (potential, spectral)


def place_tiles(spread, tiles_x, tiles_y):
    shaped = spread.reshape(tiles_x, tiles_y, 4, 2, 4, 2, KZ)
    total = 0.0
    for i in range(4):
        for j in range(4):
            part = jnp.transpose(shaped[:, :, i, :, j], (0, 2, 1, 3, 4)).reshape(
                2 * tiles_x, 2 * tiles_y, KZ
            )
            total = total + jnp.pad(part, ((2 * i, 6 - 2 * i), (2 * j, 6 - 2 * j), (0, 0)))
    return total


def gather_tiles(extended, tiles_x, tiles_y):
    blocks = []
    for i in range(4):
        members = []
        for j in range(4):
            part = extended[2 * i : 2 * i + 2 * tiles_x, 2 * j : 2 * j + 2 * tiles_y]
            part = part.reshape(tiles_x, 2, tiles_y, 2, KZ)
            members.append(jnp.transpose(part, (0, 2, 1, 3, 4)))
        blocks.append(jnp.stack(members, axis=3))
    return jnp.stack(blocks, axis=2).reshape(tiles_x, tiles_y, 64, KZ)


def local(cell_offsets, cell_z, frac, charges, tile_counts):
    block_x = KX // lax.axis_size("grp")
    block_y = KY // lax.axis_size("pen")
    tiles_x = block_x // 2
    tiles_y = block_y // 2
    slots = charges.shape[0] // (tiles_x * tiles_y)
    offsets = cell_offsets.reshape(2, tiles_x, tiles_y, slots)
    zcell = cell_z.reshape(tiles_x, tiles_y, slots)
    fracs = frac.reshape(3, tiles_x, tiles_y, slots)
    charge = charges.reshape(tiles_x, tiles_y, slots)
    counts = tile_counts.reshape(tiles_x, tiles_y)
    weight_x, grade_x, weight_y, grade_y, weight_z, grade_z, live_q = tile_weights(
        offsets, zcell, fracs, charge, counts, KZ
    )
    pair = weight_x[..., :, None, :] * weight_y[..., None, :, :] * live_q[..., None, None, :]
    pair = pair.reshape(tiles_x, tiles_y, 64, slots)
    spread = jnp.einsum("abfs,absz->abfz", pair, weight_z, precision=highest)
    padded = place_tiles(spread, tiles_x, tiles_y)
    rim_y = shifted(padded[: block_x + 5, block_y : block_y + 5], "pen", 1)
    merged = padded[: block_x + 5, :block_y].at[:, :5].add(rim_y)
    rim_x = shifted(merged[block_x : block_x + 5], "grp", 1)
    grid = merged[:block_x].at[:5].add(rim_x)
    potential, spectral = spectrum_pen_first(grid, block_x, block_y)
    upper = shifted(potential[:5], "grp", -1)
    ext_x = jnp.concatenate([potential, upper, jnp.zeros((1, block_y, KZ), jnp.float32)], axis=0)
    beside = shifted(ext_x[:, :5], "pen", -1)
    extended = jnp.concatenate(
        [ext_x, beside, jnp.zeros((block_x + 6, 1, KZ), jnp.float32)], axis=1
    )
    footing = gather_tiles(extended, tiles_x, tiles_y)
    main = jnp.einsum("abfz,absz->abfs", footing, weight_z, precision=highest).reshape(
        tiles_x, tiles_y, 8, 8, slots
    )
    tilt = jnp.einsum("abfz,absz->abfs", footing, grade_z, precision=highest).reshape(
        tiles_x, tiles_y, 8, 8, slots
    )
    force_x = -live_q * jnp.einsum(
        "abxs,abys,abxys->abs", grade_x, weight_y, main, precision=highest
    )
    force_y = -live_q * jnp.einsum(
        "abxs,abys,abxys->abs", weight_x, grade_y, main, precision=highest
    )
    force_z = -live_q * jnp.einsum(
        "abxs,abys,abxys->abs", weight_x, weight_y, tilt, precision=highest
    )
    total = lax.psum(spectral, ("grp", "pen"))
    forces = jnp.stack([force_x, force_y, force_z], axis=0).reshape(3, tiles_x * tiles_y * slots)
    return (forces, total / ATOMS)


def solution(mesh):
    in_specs = (
        P(None, ("grp", "pen")),
        P(("grp", "pen")),
        P(None, ("grp", "pen")),
        P(("grp", "pen")),
        P(("grp", "pen")),
    )
    out_specs = (P(None, ("grp", "pen")), P())
    return jax.shard_map(local, mesh=mesh, in_specs=in_specs, out_specs=out_specs, check_vma=False)
```

profile of v0, /device:TPU:8, one launch (start us, length us, event | category | flops | bytes accessed | tf_op | source)
XLA Modules:
  0.0 1137.7 jit_solution(11327651914012425456)
XLA Ops:
  14.0 3.9 select_add_fusion.4
  23.0 140.7 %fusion.15 = f32[32,16,64,256]{3,2,1,0:T(8,128)} fusion(f32[32,16,64]{2,1,0:T(8,128)S(1)} %copy-done.60, s32[32,16,64]{2,1,0:T(8,128)S(1)} %get-tuple-element.184, f32[32,16,64]{2,1,0:T(8,128)S(1)} %copy-done.58, s32[32,16,64]{2,1,0:T(8,128)S(1)} %get-tuple-element.183, f32[32,16,64]{2,1,0:T(8,128)S(1)} %copy-done.54, ...), kind=kOutput, calls=%fused_computation.27 | convolution fusion | flops 6589251584 | bytes 37355520 | tf_op jit(solution)/shard_map/abfs,absz->abfz/dot_general | solution.py:226
  163.7 39.0 %reshape.1907 = f32[32,16,4,2,4,2,256]{6,5,4,3,2,1,0:T(2,128)} reshape(f32[32,16,64,256]{3,2,1,0:T(8,128)} %fusion.15) | data formatting | bytes 67108864 | tf_op jit(solution)/shard_map/reshape | solution.py:187
  202.7 25.3 %slice_bitcast_fusion.15 = (f32[32,2,16,2,256]{4,3,1,2,0:T(2,128)S(1)}, f32[32,2,16,2,256]{4,3,1,2,0:T(2,128)S(1)}, f32[32,2,16,2,256]{4,3,1,2,0:T(2,128)}, f32[...) fusion(f32[32,16,4,2,4,2,256]{6,5,4,3,2,1,0:T(2,128)} %reshape.1907), kind=kLoop, calls=%fused_computation.93 | loop fusion | bytes 67108864 | tf_op jit(solution)/shard_map/transpose | solution.py:191
  234.0 4.0 copy.275
  241.7 4.1 copy.276
  245.8 3.8 reshape.1910
  249.6 4.0 copy.277
  253.5 3.7 reshape.1911
  257.3 4.1 copy.278
  265.0 4.0 copy.279
  272.7 4.0 copy.280
  280.4 4.0 copy.281
  288.0 4.0 copy.282
  292.1 3.9 reshape.1916
  295.9 4.0 copy.283
  303.6 4.1 copy.284
  311.3 4.0 copy.285
  315.3 3.7 reshape.1919
  319.0 4.1 copy.286
  326.8 4.0 copy.287
  330.8 3.7 reshape.1921
  334.5 4.0 copy.288
  338.5 4.0 reshape.1922
  348.6 12.9 %pad_add_fusion = f32[70,38,256]{2,0,1:T(8,128)S(1)} fusion(f32[64,32,256]{2,0,1:T(8,128)} %reshape.1923, f32[64,32,256]{2,0,1:T(8,128)} %reshape.1922, f32[64,32,256]{2,0,1:T(8,128)} %reshape.1921, f32[64,32,256]{2,0,1:T(8,128)} %reshape.1920, f32[64,32,256]{2,0,1:T(8,128)} %reshape.1919, f32[64,32,256]{2,0,1:T(8,128)} %reshape.1918, ...), kind=kLoop, calls=%fused_computation.52 | loop fusion | flops 10214400 | bytes 36278272 | tf_op jit(solution)/shard_map/add | solution.py:194
  364.9 4.5 collective-permute-done
  386.1 7.5 copy.290
  393.6 4.6 all_to_all.52
  398.6 31.3 %all_to_all.70 = f32[32,8,2176]{2,0,1:T(8,128)} all-to-all(f32[32,8,2176]{2,0,1:T(8,128)S(1)} %copy.291), channel_id=1, replica_groups=mesh['grp'=4,'pen'=8] {'pen'}, dimensions={1} | all-to-all | bytes 4456448 | tf_op jit(solution)/shard_map/all_to_all | solution.py:151
  438.6 5.1 copy.296
  443.7 5.1 copy.297
  448.8 6.2 all-to-all-start.1
  455.6 47.2 %all-to-all-done.1 = f32[64,4,2176]{2,0,1:T(8,128)S(1)} async-done(((f32[64,4,2176]{2,0,1:T(8,128)}), f32[64,4,2176]{2,0,1:T(8,128)S(1)}, u32[]{:S(2)}, u32[]{:S(2)}) %all-to-all-start.1) | async-done | bytes 2228256 | tf_op jit(solution)/shard_map/all_to_all | solution.py:156
  531.4 4.9 all_to_all.60
  536.2 4.5 copy.311
  540.8 55.5 %all_to_all.71 = f32[4,64,2176]{2,1,0:T(8,128)} all-to-all(f32[4,64,2176]{2,1,0:T(8,128)S(1)} %copy.311), channel_id=1, replica_groups=mesh['grp'=4,'pen'=8] {'grp'}, dimensions={0} | all-to-all | bytes 4456448 | tf_op jit(solution)/shard_map/all_to_all | solution.py:168
  596.3 4.7 copy.312
  601.0 7.0 copy.372
  608.0 6.1 copy.313
  614.1 4.6 fusion.36
  622.4 5.1 copy.317
  627.5 4.6 all_to_all.63
  632.1 30.6 %all_to_all.72 = f32[8,32,2176]{2,1,0:T(8,128)S(1)} all-to-all(f32[8,32,2176]{2,1,0:T(8,128)S(1)} %all_to_all.63), channel_id=1, replica_groups=mesh['grp'=4,'pen'=8] {'pen'}, dimensions={0} | all-to-all | bytes 4456448 | tf_op jit(solution)/shard_map/all_to_all | solution.py:174
  664.0 4.1 reshape.1927
  668.1 8.8 fusion.280
  676.9 5.8 copy.378
  682.8 5.3 fusion.141
  688.1 4.7 copy.377
  692.8 4.2 fusion.143
  699.5 55.4 %select_add_fusion.1.clone.4 = f32[32,16,64,256]{3,2,1,0:T(8,128)} fusion(f32[32,16,64]{2,1,0:T(8,128)S(1)} %copy-done.61, s32[32,16,64]{2,1,0:T(8,128)S(1)} %copy-done.43, f32[32,16,64]{2,1,0:T(8,128)S(1)} %copy-done.59, s32[32,16,64]{2,1,0:T(8,128)S(1)} %copy-done.41, f32[32,16,64]{2,1,0:T(8,128)S(1)} %copy-done.55, ...), kind=kLoop, calls=%fused_computation.13.clone.clone.clone.clone.1 | loop fusion | flops 142606336 | bytes 35127296 | tf_op jit(solution)/shard_map/abxs,abys,abxys->abs/dot_general | solution.py:246
  756.3 55.3 %fusion.294 = f32[32,16,64,256]{3,2,1,0:T(8,128)} fusion(f32[32,16,64]{2,1,0:T(8,128)S(1)} %copy-done.53, f32[32,16,64]{2,1,0:T(8,128)S(1)} %copy-done.51, f32[32,16,64]{2,1,0:T(8,128)S(1)} %copy-done.50, f32[32,16,64]{2,1,0:T(8,128)S(1)} %copy-done.52, f32[32,16,64]{2,1,0:T(8,128)S(1)} %copy-done.49, f32[32,16,64]{2,1,0:T(8,128)S(1)} %copy-done.48, ...), kind=kLoop, calls=%fused_computation.2.clone.clone.clone.1 | loop fusion | flops 142606336 | bytes 35127296 | tf_op jit(solution)/shard_map/abfz,absz->abfs/dot_general | solution.py:243
  812.3 39.4 %psum.7 = f32[]{:T(128)} all-reduce(f32[]{:T(128)S(6)} %mul_shard_map.3), channel_id=1, replica_groups=mesh['grp'=4,'pen'=8] {'grp','pen'}, use_global_device_ids=true, to_apply=%region_1.6 | all-reduce | flops 1 | bytes 8 | tf_op jit(solution)/shard_map/psum | solution.py:255
  868.1 6.2 fusion.282
  905.4 3.8 reshape.1941
  915.0 6.8 maximum_bitcast_fusion
  921.9 4.5 maximum_bitcast_fusion.1
  926.4 5.3 maximum_bitcast_fusion.2
  932.8 5.2 maximum_bitcast_fusion.3
  938.0 18.5 %pad_maximum_fusion = f32[32,16,4,2,4,2,256]{6,3,0,5,1,4,2:T(2,128)} fusion(f32[32,16,1,2,4,2,256]{6,3,0,5,1,4,2:T(2,128)} %maximum_bitcast_fusion.3, f32[32,16,1,2,4,2,256]{6,3,0,5,1,4,2:T(2,128)} %maximum_bitcast_fusion.2, f32[32,16,1,2,4,2,256]{6,3,0,5,1,4,2:T(2,128)S(1)} %maximum_bitcast_fusion.1, f32[32,16,1,2,4,2,256]{6,3,0,5,1,4,2:T(2,128)S(1)} %maximum_bitcast_fusion), kind=kLoop, calls=%fused_computation | loop fusion | flops 25165824 | bytes 67108864 | tf_op jit(solution)/shard_map/stack | solution.py:207
  956.5 46.1 %copy.321 = f32[32,16,4,2,4,2,256]{6,5,4,3,2,1,0:T(2,128)} copy(f32[32,16,4,2,4,2,256]{6,3,0,5,1,4,2:T(2,128)} %pad_maximum_fusion) | data formatting | bytes 67108864 | tf_op jit(solution)/shard_map/stack | solution.py:207
  1002.6 39.9 %reshape.1944 = f32[32,16,64,256]{3,2,1,0:T(8,128)} reshape(f32[32,16,4,2,4,2,256]{6,5,4,3,2,1,0:T(2,128)} %copy.321) | data formatting | bytes 67108864 | tf_op jit(solution)/shard_map/reshape | solution.py:207
  1042.5 42.5 %fusion.12 = f32[32,16,64,8]{2,3,1,0:T(8,128)} fusion(f32[32,16,64,8]{2,3,1,0:T(8,128)S(1)} %bitcast.442, f32[32,16,64,256]{3,2,1,0:T(8,128)} %reshape.1944, f32[32,16,64,256]{3,2,1,0:T(8,128)} %fusion.294), kind=kOutput, calls=%fused_computation.21 | convolution fusion | flops 6446383104 | bytes 69206016 | tf_op jit(solution)/shard_map/abfz,absz->abfs/dot_general | solution.py:243
  1085.0 41.7 %fusion.13 = (f32[32,16,64,8]{2,3,1,0:T(8,128)}, f32[32,16,64,8]{2,3,1,0:T(8,128)}) fusion(f32[32,16,64,8]{2,3,1,0:T(8,128)} %get-tuple-element.128, f32[32,16,64,8]{2,3,1,0:T(8,128)S(1)} %bitcast.443, f32[32,16,64,256]{3,2,1,0:T(8,128)} %reshape.1944, f32[32,16,64,256]{3,2,1,0:T(8,128)} %select_add_fusion.1.clone.4), kind=kOutput, calls=%fused_computation.24 | convolution fusion | flops 6450315264 | bytes 71303168 | tf_op jit(solution)/shard_map/abfz,absz->abfs/dot_general | solution.py:240
  1126.8 4.9 multiply_reduce_fusion.2
  (311 shorter events, 184.4 us)
Async XLA Ops:
  13.3 8.3 copy-start.32
  13.3 8.3 copy-start.34
  13.3 8.3 copy-start.36
  13.3 8.3 copy-start.38
  13.4 8.3 copy-start.40
  13.4 8.3 copy-start.42
  13.5 4.3 copy-start.44
  13.6 4.3 copy-start.90
  13.8 4.1 copy-start.47
  13.8 4.1 copy-start.66
  13.8 4.1 copy-start.67
  13.8 4.1 copy-start.68
  13.8 4.1 copy-start.69
  13.8 4.1 copy-start.70
  13.8 4.1 copy-start.71
  13.9 4.1 copy-start.72
  13.9 4.1 copy-start.73
  13.9 4.1 copy-start.74
  13.9 4.1 copy-start.75
  13.9 4.1 copy-start.76
  13.9 4.1 copy-start.77
  13.9 4.1 copy-start.78
  13.9 4.1 copy-start.79
  13.9 4.1 copy-start.80
  13.9 4.1 copy-start.81
  14.0 4.1 copy-start.82
  18.0 4.9 copy-start.54
  18.0 4.9 copy-start.56
  18.0 4.9 copy-start.58
  18.1 4.9 copy-start.60
  18.1 4.9 copy-start.62
  18.1 4.9 copy-start.64
  361.5 7.9 collective-permute-start
  371.2 6.5 collective-permute-start.1
  448.8 53.9 %all-to-all-start.1 = ((f32[64,4,2176]{2,0,1:T(8,128)}), f32[64,4,2176]{2,0,1:T(8,128)S(1)}, u32[]{:S(2)}, u32[]{:S(2)}) async-start(f32[64,4,2176]{2,0,1:T(8,128)} %copy.297), calls=%async_computation.1 | async-start | bytes 4456448 | tf_op jit(solution)/shard_map/all_to_all | solution.py:156
  692.8 4.3 copy-start.6
  697.6 57.4 %collective-permute-start.2 = (f32[5,32,256]{2,0,1:T(8,128)S(1)}, f32[5,32,256]{2,0,1:T(8,128)S(1)}, u32[]{:S(2)}, u32[]{:S(2)}) collective-permute-start(f32[5,32,256]{2,0,1:T(8,128)S(1)} %slice.369), channel_id=1, source_target_pairs={{8,0},{16,8},{24,16},{0,24},{9,1},{17,9},{25,17},{1,25},{10,2},{18... | collective-permute-start | bytes 491528 | tf_op jit(solution)/shard_map/ppermute | solution.py:21
  755.1 112.8 %collective-permute-start.3 = (f32[70,5,256]{2,0,1:T(8,128)S(1)}, f32[70,5,256]{2,0,1:T(8,128)S(1)}, u32[]{:S(2)}, u32[]{:S(2)}) collective-permute-start(f32[70,5,256]{2,0,1:T(8,128)S(1)} %pad_maximum_fusion.10), channel_id=1, source_target_pairs={{1,0},{2,1},{3,2},{4,3},{5,4},{6,5},{7,6},{0,7},{9,8},{10,9},{11,1... | collective-permute-start | bytes 1075208 | tf_op jit(solution)/shard_map/ppermute | solution.py:21
  915.0 6.8 copy-start.10
  915.0 6.8 copy-start.11
  915.0 6.8 copy-start.12
  915.0 6.8 copy-start.14
  921.8 4.5 copy-start.8
  921.9 4.5 copy-start.13
  921.9 4.5 copy-start.15
  921.9 4.5 copy-start.17
  926.4 5.3 copy-start.7
  926.4 5.3 copy-start.16
  926.4 5.6 copy-start.18
  926.4 6.4 copy-start.19
  1002.6 39.9 %copy-start.1 = (f32[32,16,8,64]{3,2,1,0:T(8,128)S(1)}, f32[32,16,8,64]{3,2,1,0:T(8,128)}, u32[]{:S(2)}) copy-start(f32[32,16,8,64]{3,2,1,0:T(8,128)} %copy-done) | copy-start | bytes 3145732
  1085.0 41.7 %copy-start.21 = (s32[32,16,64]{2,1,0:T(8,128)S(1)}, s32[32,16,64]{2,1,0:T(8,128)}, u32[]{:S(2)}) copy-start(s32[32,16,64]{2,1,0:T(8,128)} %copy-done.20) | copy-start | bytes 393220
  1085.0 41.7 %copy-start.23 = (s32[32,16,64]{2,1,0:T(8,128)S(1)}, s32[32,16,64]{2,1,0:T(8,128)}, u32[]{:S(2)}) copy-start(s32[32,16,64]{2,1,0:T(8,128)} %copy-done.22) | copy-start | bytes 393220
  1085.0 41.7 %copy-start.25 = (s32[32,16,64]{2,1,0:T(8,128)S(1)}, s32[32,16,64]{2,1,0:T(8,128)}, u32[]{:S(2)}) copy-start(s32[32,16,64]{2,1,0:T(8,128)} %copy-done.24) | copy-start | bytes 393220
  1085.0 41.7 %copy-start.27 = (s32[32,16,64]{2,1,0:T(8,128)S(1)}, s32[32,16,64]{2,1,0:T(8,128)}, u32[]{:S(2)}) copy-start(s32[32,16,64]{2,1,0:T(8,128)} %copy-done.26) | copy-start | bytes 393220
  1085.0 41.7 %copy-start.29 = (s32[32,16,64]{2,1,0:T(8,128)S(1)}, s32[32,16,64]{2,1,0:T(8,128)}, u32[]{:S(2)}) copy-start(s32[32,16,64]{2,1,0:T(8,128)} %copy-done.28) | copy-start | bytes 393220
  1126.7 4.9 copy-start.4
  1126.7 4.9 copy-start.31
  1126.7 4.9 copy-start.83
  1126.7 4.9 copy-start.84
  1126.8 4.9 copy-start.85
  1126.8 4.9 copy-start.86
  1126.8 4.9 copy-start.87
  1126.8 4.9 copy-start.88
  (36 other events, 90.7 us)
where the time goes:
time: 1150 us; the launch traced here: 1140 us
  local copies, waits for them, and re-layouts  446 us (39%)
  matrix products  265 us (23%)
  other arithmetic  201 us (17%)
  blocking collectives  157 us (14%)
  waiting for transfers between devices  54.6 us (5%)
    dot_general x1, matrix products, local(): spread = jnp.einsum('abfs,absz->abfz', pair, weight_z, precision=highest)  141 us
    transpose x17, local copies, waits for them, and re-layouts, place_tiles(): jnp.transpose(shaped[:, :, i, :, j], (0, 2, 1, 3, 4))  86.3 us
    dot_general x2, other arithmetic, local(): jnp.einsum('abxs,abys,abxys->abs', grade_x, weight_y, main, precision=hig...  60.3 us
    reshape x16, local copies, waits for them, and re-layouts, place_tiles(): jnp.transpose(shaped[:, :, i, :, j], (0, 2, 1, 3, 4))  59.5 us
    all_to_all x1, blocking collectives, spectrum_pen_first(): lax.all_to_all(returning, 'grp', split_axis=0, concat_axis=1, tiled=True)  55.5 us
    dot_general x1, other arithmetic, local(): jnp.einsum('abfz,absz->abfs', footing, grade_z, precision=highest)  55.3 us
    reshape x16, local copies, waits for them, and re-layouts, gather_tiles(): part = part.reshape(tiles_x, 2, tiles_y, 2, KZ)  50 us
    all_to_all x1, waiting for transfers between devices, spectrum_pen_first(): lax.all_to_all(sectioned, 'grp', split_axis=1, concat_axis=0, tiled=True)  47.2 us
  transfers between devices with their start and end apart: 5, of which 3 were waited for; matrix products, arithmetic and copies ran while one was open for 12% of the time, Pallas kernels for 0%

commit v1 on v0

--- a/solution.py
+++ b/solution.py
@@ -2,17 +2,24 @@
 
 import jax
 import jax.numpy as jnp
+import numpy as np
 from jax import lax
+from jax.experimental import pallas as pl
+from jax.experimental.pallas import tpu as pltpu
 from jax.sharding import PartitionSpec as P
 
 KX = 256
 KY = 256
 KZ = 256
-ATOMS = 1048576
-
+LANES = 128
+ROWS = 16
+SPAN = 7
+REACH = 5
 
 ewald_split = 0.6
 highest = lax.Precision.HIGHEST
+f32 = jnp.float32
+bf16 = jnp.bfloat16
 
 
 def shifted(block, axis, distance):
@@ -21,58 +28,530 @@
     return lax.ppermute(block, axis, route)
 
 
-def spline_rows(fracs):
-    values = [jnp.ones_like(fracs)]
-    fifth = values
+def shifted_both(block, distance):
+    groups, pens = lax.axis_size("grp"), lax.axis_size("pen")
+    route = []
+    for g in range(groups):
+        for p in range(pens):
+            source = ((g - distance) % groups) * pens + (p - distance) % pens
+            route.append((source, g * pens + p))
+    return lax.ppermute(block, ("grp", "pen"), route)
+
+
+def halves(value):
+    high = value.astype(bf16)
+    low = (value - high.astype(f32)).astype(bf16)
+    return high, low
+
+
+def table_halves(table):
+    table = jnp.asarray(np.asarray(table, np.float32))
+    return halves(table)
+
+
+def dot(left, right, dims):
+    return lax.dot_general(left, right, (dims, ((), ())), preferred_element_type=f32)
+
+
+NN = ((1,), (0,))
+NT = ((1,), (1,))
+
+
+def spline_rows(x):
+    values = [jnp.ones_like(x)]
+    fifth = None
     for order in range(2, 7):
         nxt = []
         for j in range(order):
-            term = jnp.zeros_like(fracs)
+            term = None
             if j >= 1:
-                term = values[j - 1] * (fracs + order - 1 - j)
+                term = values[j - 1] * (x + float(order - 1 - j))
             if j <= order - 2:
-                term = term + values[j] * (1.0 - fracs + j)
-            nxt.append(term / (order - 1))
+                other = values[j] * (float(1 + j) - x)
+                term = other if term is None else term + other
+            nxt.append(term)
         if order == 5:
-            fifth = nxt
+            fifth = [v * (1.0 / 24.0) for v in nxt]
         values = nxt
-    slopes = []
-    for j in range(6):
-        term = jnp.zeros_like(fracs)
-        if j >= 1:
-            term = fifth[j - 1]
-        if j <= 4:
-            term = term - fifth[j]
-        slopes.append(term)
-    return (values, slopes)
-
-
-def tile_weights(offsets, zcell, fracs, charge, counts, size_z):
-    slots = charge.shape[-1]
-    live = (jnp.arange(slots, dtype=jnp.int32) < counts[..., None]).astype(jnp.float32)
-    live_q = charge * live
-    theta_x, slope_x = spline_rows(fracs[0])
-    theta_y, slope_y = spline_rows(fracs[1])
-    theta_z, slope_z = spline_rows(fracs[2])
-    footing = jnp.arange(8, dtype=jnp.int32)[:, None]
-    cells = jnp.arange(size_z, dtype=jnp.int32)
-    weight_x = 0.0
-    grade_x = 0.0
-    weight_y = 0.0
-    grade_y = 0.0
-    weight_z = 0.0
-    grade_z = 0.0
-    for j in range(6):
-        hit_x = (footing == offsets[0][..., None, :] + j).astype(jnp.float32)
-        hit_y = (footing == offsets[1][..., None, :] + j).astype(jnp.float32)
-        hit_z = (cells == (zcell[..., :, None] + j) % size_z).astype(jnp.float32)
-        weight_x = weight_x + theta_x[j][..., None, :] * hit_x
-        grade_x = grade_x + slope_x[j][..., None, :] * hit_x
-        weight_y = weight_y + theta_y[j][..., None, :] * hit_y
-        grade_y = grade_y + slope_y[j][..., None, :] * hit_y
-        weight_z = weight_z + theta_z[j][..., :, None] * hit_z
-        grade_z = grade_z + slope_z[j][..., :, None] * hit_z
-    return (weight_x, grade_x, weight_y, grade_y, weight_z, grade_z, live_q)
+    thetas = [v * (1.0 / 120.0) for v in values]
+    slopes = [-fifth[0]]
+    for j in range(1, 5):
+        slopes.append(fifth[j - 1] - fifth[j])
+    slopes.append(fifth[4])
+    return thetas, slopes
+
+
+def placed(rows, offset):
+    out = []
+    zero = jnp.zeros_like(rows[0])
+    for i in range(SPAN):
+        here = rows[i] if i <= 5 else zero
+        before = rows[i - 1] if i >= 1 else zero
+        out.append(jnp.where(offset == 0, here, before))
+    return out
+
+
+def spread_out(row):
+    return jnp.broadcast_to(row, (ROWS, row.shape[-1]))
+
+
+def live_charges(q_ref, counts_ref, step, slots):
+    per_row = LANES // slots
+    row_at = lax.broadcasted_iota(jnp.int32, (8, LANES), 0)
+    lane_at = lax.broadcasted_iota(jnp.int32, (8, LANES), 1)
+    tile_at = row_at * per_row + lane_at // slots
+    count = jnp.zeros((8, LANES), jnp.int32)
+    for k in range(8 * per_row):
+        count = jnp.where(tile_at == k, counts_ref[step * (8 * per_row) + k], count)
+    charge = q_ref[pl.ds(pl.multiple_of(step * 8, 8), 8), :]
+    return jnp.where(lane_at % slots < count, charge, 0.0)
+
+
+def step_rows(step, frac_ref, offs_ref, z_ref, slots):
+    rows = pl.ds(pl.multiple_of(step * 8, 8), 8)
+    fracs = [frac_ref[d, rows, :] for d in range(3)]
+    offset_x = offs_ref[0, rows, :]
+    offset_y = offs_ref[1, rows, :]
+    row_at = lax.broadcasted_iota(jnp.int32, (8, LANES), 0)
+    lane_at = lax.broadcasted_iota(jnp.int32, (8, LANES), 1)
+    per_row = LANES // slots
+    tile_in_group = (row_at % 2) * per_row + lane_at // slots
+    offset_y = offset_y + 2 * tile_in_group
+    return fracs, offset_x, offset_y, z_ref[rows, :]
+
+
+def by_distance(distance, rows, row):
+    out = jnp.where(distance == 0, spread_out(rows[0][row]), 0.0)
+    for j in range(1, 6):
+        out = jnp.where(distance == j, spread_out(rows[j][row]), out)
+    return out
+
+
+def z_parts(zcell, row, lists):
+    cell = spread_out(zcell[row])
+    at = lax.broadcasted_iota(jnp.int32, (ROWS, LANES), 0)
+    ahead = (at - cell) & (ROWS - 1)
+    block = ((cell + ahead) & (KZ - 1)) // ROWS
+    weights = [by_distance(ahead, rows, row) for rows in lists]
+    return block.astype(f32).astype(bf16), weights
+
+
+def z_matrix(block, weight):
+    zero = jnp.zeros_like(weight)
+    return jnp.concatenate(
+        [jnp.where(block == jnp.array(k, bf16), weight, zero) for k in range(KZ // ROWS)], axis=0
+    )
+
+
+def group_place(step, k, groups):
+    index = step * 4 + k
+    return index // groups, index % groups
+
+
+def spread_body(
+    counts_ref, frac_ref, offs_ref, z_ref, q_ref, core_ref, rim_y_ref, rim_x_ref, corner_ref, acc_ref,
+    *, slots, groups, block_x, block_y,
+):
+    acc_ref[...] = jnp.zeros_like(acc_ref)
+    at = lax.broadcasted_iota(jnp.int32, (ROWS, LANES), 0)
+
+    def body(step, carry):
+        fracs, offset_x, offset_y, zcell = step_rows(step, frac_ref, offs_ref, z_ref, slots)
+        charge = live_charges(q_ref, counts_ref, step, slots)
+        theta_x, _ = spline_rows(fracs[0])
+        theta_y, _ = spline_rows(fracs[1])
+        theta_z, _ = spline_rows(fracs[2])
+        theta_y = [t * charge for t in theta_y]
+        weight_x = placed(theta_x, offset_x)
+        for k in range(4):
+            blocks, zs, pairs = [], [], []
+            for half in range(2):
+                row = slice(2 * k + half, 2 * k + half + 1)
+                block, (weight,) = z_parts(zcell, row, [theta_z])
+                blocks.append(block)
+                zs.append(weight)
+                weight_y = by_distance(at - spread_out(offset_y[row]), theta_y, row)
+                pairs.append([spread_out(weight_x[i][row]) * weight_y for i in range(SPAN)])
+            block = jnp.concatenate(blocks, axis=1)
+            z_high, z_low = halves(jnp.concatenate(zs, axis=1))
+            table_high = z_matrix(block, z_high)
+            table_low = z_matrix(block, z_low)
+            pair = jnp.concatenate(
+                [jnp.concatenate([pairs[0][i], pairs[1][i]], axis=1) for i in range(SPAN)], axis=0
+            )
+            high, low = halves(pair)
+            both = dot(jnp.concatenate([high, low], axis=0), table_high, NT)
+            rest = dot(high, table_low, NT)
+            total = both[: SPAN * ROWS] + both[SPAN * ROWS :] + rest
+            a, g = group_place(step, k, groups)
+            where = (pl.ds(2 * a, SPAN), pl.ds(pl.multiple_of(8 * g, 8), ROWS))
+            acc_ref[where[0], where[1], :] += total.reshape(SPAN, ROWS, KZ)
+        return carry
+
+    lax.fori_loop(0, frac_ref.shape[1] // 8, body, 0)
+    core_ref[...] = acc_ref[:block_x, :block_y, :]
+    rim_y_ref[...] = acc_ref[:block_x, block_y : block_y + 8, :]
+    rim_x_ref[...] = acc_ref[block_x : block_x + REACH, :block_y, :]
+    corner_ref[...] = acc_ref[block_x : block_x + REACH, block_y : block_y + 8, :]
+
+
+vmem = pl.BlockSpec(memory_space=pltpu.VMEM)
+smem = pl.BlockSpec(memory_space=pltpu.SMEM)
+
+
+def spread_charges(counts, frac, offs, zcell, charge, slots, groups, block_x, block_y):
+    import functools
+
+    body = functools.partial(spread_body, slots=slots, groups=groups, block_x=block_x, block_y=block_y)
+    shapes = [
+        (block_x, block_y, KZ), (block_x, 8, KZ), (REACH, block_y, KZ), (REACH, 8, KZ),
+    ]
+    return pl.pallas_call(
+        body,
+        out_shape=[jax.ShapeDtypeStruct(s, f32) for s in shapes],
+        in_specs=[smem] + [vmem] * 4,
+        out_specs=[vmem] * 4,
+        scratch_shapes=[pltpu.VMEM((block_x + REACH, block_y + 8, KZ), f32)],
+        name="spread",
+    )(counts, frac, offs, zcell, charge)
+
+
+def interp_body(
+    counts_ref, frac_ref, offs_ref, z_ref, q_ref, core_ref, rim_y_ref, rim_x_ref, corner_ref, out_ref, pot_ref,
+    *, slots, groups, block_x, block_y,
+):
+    pot_ref[:block_x, :block_y, :] = core_ref[...]
+    pot_ref[:block_x, block_y : block_y + 8, :] = rim_y_ref[...]
+    pot_ref[block_x : block_x + REACH, :block_y, :] = rim_x_ref[...]
+    pot_ref[block_x : block_x + REACH, block_y : block_y + 8, :] = corner_ref[...]
+    at = lax.broadcasted_iota(jnp.int32, (ROWS, LANES), 0)
+    height = SPAN * ROWS
+
+    def body(step, carry):
+        fracs, offset_x, offset_y, zcell = step_rows(step, frac_ref, offs_ref, z_ref, slots)
+        charge = live_charges(q_ref, counts_ref, step, slots)
+        theta_x, slope_x = spline_rows(fracs[0])
+        theta_y, slope_y = spline_rows(fracs[1])
+        theta_z, slope_z = spline_rows(fracs[2])
+        theta_y = [t * -charge for t in theta_y]
+        slope_y = [t * -charge for t in slope_y]
+        weight_x = placed(theta_x, offset_x)
+        grade_x = placed(slope_x, offset_x)
+        rows_out = [[], [], []]
+        for k in range(4):
+            blocks, zs, gs = [], [], []
+            for half in range(2):
+                row = slice(2 * k + half, 2 * k + half + 1)
+                block, (weight, grade) = z_parts(zcell, row, [theta_z, slope_z])
+                blocks.append(block)
+                zs.append(weight)
+                gs.append(grade)
+            block = jnp.concatenate(blocks, axis=1)
+            z_high, z_low = halves(jnp.concatenate(zs, axis=1))
+            g_high, g_low = halves(jnp.concatenate(gs, axis=1))
+            a, g = group_place(step, k, groups)
+            slab = pot_ref[pl.ds(2 * a, SPAN), pl.ds(pl.multiple_of(8 * g, 8), ROWS), :]
+            high, low = halves(slab.reshape(height, KZ))
+            stacked = jnp.concatenate([high, low], axis=0)
+            main = dot(stacked, z_matrix(block, z_high), NN)
+            main = main[:height] + main[height:] + dot(high, z_matrix(block, z_low), NN)
+            tilt = dot(stacked, z_matrix(block, g_high), NN)
+            tilt = tilt[:height] + tilt[height:] + dot(high, z_matrix(block, g_low), NN)
+            for half in range(2):
+                row = slice(2 * k + half, 2 * k + half + 1)
+                lanes = slice(half * LANES, (half + 1) * LANES)
+                away = at - spread_out(offset_y[row])
+                weight_y = by_distance(away, theta_y, row)
+                grade_y = by_distance(away, slope_y, row)
+                plain = steep = tilted = 0.0
+                for i in range(SPAN):
+                    part = slice(i * ROWS, (i + 1) * ROWS)
+                    wide = spread_out(weight_x[i][row])
+                    plain = plain + wide * main[part, lanes]
+                    tilted = tilted + wide * tilt[part, lanes]
+                    steep = steep + spread_out(grade_x[i][row]) * main[part, lanes]
+                rows_out[0].append(jnp.sum(steep * weight_y, axis=0, keepdims=True))
+                rows_out[1].append(jnp.sum(plain * grade_y, axis=0, keepdims=True))
+                rows_out[2].append(jnp.sum(tilted * weight_y, axis=0, keepdims=True))
+        for d in range(3):
+            out_ref[d, pl.ds(pl.multiple_of(step * 8, 8), 8), :] = jnp.concatenate(rows_out[d], axis=0)
+        return carry
+
+    lax.fori_loop(0, frac_ref.shape[1] // 8, body, 0)
+
+
+def interpolate(counts, frac, offs, zcell, charge, core, rims, slots, groups, block_x, block_y):
+    import functools
+
+    body = functools.partial(interp_body, slots=slots, groups=groups, block_x=block_x, block_y=block_y)
+    return pl.pallas_call(
+        body,
+        out_shape=jax.ShapeDtypeStruct(frac.shape, f32),
+        in_specs=[smem] + [vmem] * 8,
+        out_specs=vmem,
+        scratch_shapes=[pltpu.VMEM((block_x + REACH, block_y + 8, KZ), f32)],
+        name="interpolate",
+    )(counts, frac, offs, zcell, charge, core, *rims)
+
+
+def angles(left, right, length):
+    return (np.outer(left, right) % length) * (2.0 * math.pi / length)
+
+
+def np_modulus(length):
+    index = np.arange(length)
+    coeffs = (1.0 / 120.0, 26.0 / 120.0, 66.0 / 120.0, 26.0 / 120.0, 1.0 / 120.0)
+    total = 0.0
+    for j in range(5):
+        total = total + coeffs[j] * np.exp(2j * math.pi * ((index * j) % length) / length)
+    return np.abs(total) ** 2
+
+
+def np_line(length):
+    index = np.arange(length)
+    freq = np.where(2 * index < length, index, index - length) / length
+    square = freq * freq
+    return square, np.exp(-(math.pi**2) * square / ewald_split**2) / np_modulus(length)
+
+
+def z_table(devices):
+    per = KZ // 2 // devices
+    position = np.arange(KZ)
+    forward, back = [], []
+    for device in range(devices):
+        for imaginary in range(2):
+            for plane in range(device * per, (device + 1) * per):
+                wave = 2.0 * math.pi * ((plane * position) % KZ) / KZ
+                if plane == 0:
+                    row = np.where(position % 2 == 0, 1.0, -1.0) if imaginary else np.ones(KZ)
+                    forward.append(row)
+                    back.append(row)
+                else:
+                    row = -np.sin(wave) if imaginary else np.cos(wave)
+                    forward.append(row)
+                    back.append(2.0 * row)
+    return np.stack(forward), np.stack(back)
+
+
+def forward_z_body(core_ref, rim_y_ref, rim_x_ref, corner_ref, high_ref, low_ref, out_ref, *, chunk):
+    block_x, block_y = core_ref.shape[:2]
+    high = high_ref[...]
+    low = low_ref[...]
+    stacked = jnp.concatenate([high, low], axis=0)
+    size = high.shape[0]
+    for start in range(0, block_x, chunk):
+        part = core_ref[start : start + chunk]
+        edge = part[:, :8] + rim_y_ref[start : start + chunk]
+        if start < REACH:
+            count = min(REACH - start, chunk)
+            side = rim_x_ref[start : start + count]
+            fix = side[:, :8] + corner_ref[start : start + count]
+            edge = jnp.concatenate([edge[:count] + fix, edge[count:]], axis=0)
+            rest = jnp.concatenate([part[:count, 8:] + side[:, 8:], part[count:, 8:]], axis=0)
+        else:
+            rest = part[:, 8:]
+        part = jnp.concatenate([edge, rest], axis=1).reshape(chunk * block_y, KZ)
+        part_high, part_low = halves(part)
+        both = dot(stacked, part_high, NT)
+        total = both[:size] + both[size:] + dot(high, part_low, NT)
+        out_ref[:, start * block_y : (start + chunk) * block_y] = total
+
+
+def forward_z(core, rims, high, low):
+    import functools
+
+    block_x, block_y = core.shape[:2]
+    chunk = 256 // block_y
+    return pl.pallas_call(
+        functools.partial(forward_z_body, chunk=chunk),
+        out_shape=jax.ShapeDtypeStruct((KZ, block_x * block_y), f32),
+        in_specs=[vmem] * 6,
+        out_specs=vmem,
+        name="forward_z",
+    )(core, *rims, high, low)
+
+
+def backward_z_body(in_ref, high_ref, low_ref, core_ref, rim_y_ref, rim_x_ref, corner_ref, energy_ref, *, chunk):
+    block_x, block_y = core_ref.shape[:2]
+    high = high_ref[...]
+    low = low_ref[...]
+    for start in range(0, block_x, chunk):
+        part = in_ref[:, start * block_y : (start + chunk) * block_y].T
+        part_high, part_low = halves(part)
+        size = part.shape[0]
+        both = dot(jnp.concatenate([part_high, part_low], axis=0), high, NN)
+        total = both[:size] + both[size:] + dot(part_high, low, NN)
+        total = total.reshape(chunk, block_y, KZ)
+        core_ref[start : start + chunk] = total
+        rim_y_ref[start : start + chunk] = total[:, :8]
+        if start < REACH:
+            count = min(REACH - start, chunk)
+            rim_x_ref[start : start + count] = total[:count]
+            corner_ref[start : start + count] = total[:count, :8]
+    tail = in_ref[:, block_x * block_y :]
+    energy_ref[...] = jnp.sum(tail.reshape(-1, 8, LANES), axis=0)
+
+
+def backward_z(spectral, high, low, block_x, block_y):
+    import functools
+
+    chunk = 256 // block_y
+    shapes = [
+        (block_x, block_y, KZ), (block_x, 8, KZ), (REACH, block_y, KZ), (REACH, 8, KZ), (8, LANES),
+    ]
+    return pl.pallas_call(
+        functools.partial(backward_z_body, chunk=chunk),
+        out_shape=[jax.ShapeDtypeStruct(s, f32) for s in shapes],
+        in_specs=[vmem] * 3,
+        out_specs=[vmem] * 5,
+        name="backward_z",
+    )(spectral, high, low)
+
+
+def swap_blocks(parts, width):
+    lane_at = lax.broadcasted_iota(jnp.int32, parts[0].shape, 1)
+    first = lane_at < 2 * width
+    even = (lane_at // width) % 2 == 0
+    a, b, c, d = parts
+    a, c = jnp.where(first, a, pltpu.roll(c, 2 * width, 1)), jnp.where(first, pltpu.roll(a, 2 * width, 1), c)
+    b, d = jnp.where(first, b, pltpu.roll(d, 2 * width, 1)), jnp.where(first, pltpu.roll(b, 2 * width, 1), d)
+    back = LANES - width
+    a, b = jnp.where(even, a, pltpu.roll(b, width, 1)), jnp.where(even, pltpu.roll(a, back, 1), b)
+    c, d = jnp.where(even, c, pltpu.roll(d, width, 1)), jnp.where(even, pltpu.roll(c, back, 1), d)
+    return [a, b, c, d]
+
+
+def planes_body(
+    where_ref, line_ref, in_ref, y_high_ref, y_low_ref, x_high_ref, x_low_ref, factor_ref, square_ref,
+    out_ref, main_ref, twin_ref,
+    *, pens, block_x, block_y,
+):
+    groups = KX // block_x
+    high_x = block_x * block_y // LANES
+    me = where_ref[0]
+    y_high = y_high_ref[...]
+    y_low = y_low_ref[...]
+    step_rows_count = 256
+
+    def times_y(rows):
+        high, low = halves(rows)
+        size = rows.shape[0]
+        both = dot(jnp.concatenate([high, low], axis=0), y_high, NN)
+        total = both[:size] + both[size:] + dot(high, y_low, NN)
+        turned = pltpu.roll(total[:, KY:].reshape(size // 8, 8, KY), 4, 1).reshape(size, KY)
+        return total[:, :KY], turned
+
+    comp_at = lax.broadcasted_iota(jnp.int32, (step_rows_count, KY), 0) % 8
+    sign = jnp.where(comp_at < 4, 1.0, -1.0)
+    per_step = step_rows_count // 32
+
+    def forward_step(step, carry):
+        group = step // (high_x // per_step)
+        first = (step % (high_x // per_step)) * per_step
+        rows = []
+        for k in range(per_step):
+            lanes = pl.ds(pl.multiple_of((first + k) * LANES, LANES), LANES)
+            lower = swap_blocks([in_ref[group * pens + p, :, lanes] for p in range(4)], block_y)
+            upper = swap_blocks([in_ref[group * pens + 4 + p, :, lanes] for p in range(4)], block_y)
+            for low, up in zip(lower, upper):
+                rows.append(jnp.concatenate([low, up], axis=1))
+        plain, turned = times_y(jnp.concatenate(rows, axis=0))
+        at = pl.ds(pl.multiple_of(step * step_rows_count, step_rows_count), step_rows_count)
+        main = plain + sign * turned
+        twin = sign * plain - turned
+        for k in range(2):
+            side = slice(k * LANES, (k + 1) * LANES)
+            main_ref[k, at, :] = main[:, side]
+            twin_ref[k, at, :] = twin[:, side]
+        return carry
+
+    lax.fori_loop(0, groups * high_x // per_step, forward_step, 0)
+
+    def times_x(real, imag):
+        high, low = halves(jnp.concatenate([real, imag], axis=0))
+        x_high = x_high_ref[...]
+        total = dot(x_high, high, NN) + dot(x_high, low, NN) + dot(x_low_ref[...], high, NN)
+        return total[:KX], total[KX:]
+
+    def plane_of(ref, comp):
+        return jnp.concatenate([ref[k, pl.ds(comp, KX, stride=8), :] for k in range(2)], axis=1)
+
+    def influence(entry):
+        square = square_ref[...] + line_ref[0, entry]
+        value = factor_ref[...] * line_ref[1, entry] / jnp.where(square > 0, square, 1.0)
+        return jnp.where(square > 0, value, 0.0)
+
+    energy = jnp.zeros((KX, KY), f32)
+    for plane in range(4):
+        real, imag = times_x(plane_of(main_ref, plane), plane_of(main_ref, plane + 4))
+        kernel = influence(me * 4 + plane)
+        if plane == 0:
+            mine = me == 0
+            other = influence(KZ // 2)
+            share = jnp.where(mine, 0.5 * (kernel + other), kernel)
+            cross = jnp.where(mine, 0.5 * (kernel - other), 0.0)
+            twin_real, twin_imag = times_x(plane_of(twin_ref, 0), plane_of(twin_ref, 4))
+            out_real = share * real + cross * twin_real
+            out_imag = share * imag + cross * twin_imag
+            energy = energy + jnp.where(mine, 0.5, 1.0) * (real * out_real + imag * out_imag)
+        else:
+            out_real = kernel * real
+            out_imag = kernel * imag
+            energy = energy + (real * out_real + imag * out_imag)
+        real, imag = times_x(out_real, -out_imag)
+        for k in range(2):
+            side = slice(k * LANES, (k + 1) * LANES)
+            main_ref[k, pl.ds(plane, KX, stride=8), :] = real[:, side]
+            main_ref[k, pl.ds(plane + 4, KX, stride=8), :] = -imag[:, side]
+
+    total = jnp.sum(jnp.sum(energy, axis=0, keepdims=True), axis=1, keepdims=True)
+    out_ref[:, :, block_x * block_y :] = jnp.broadcast_to(
+        total.reshape(1, 1, 1), (groups * pens, 8, LANES)
+    )
+
+    def backward_step(step, carry):
+        group = step // (high_x // per_step)
+        first = (step % (high_x // per_step)) * per_step
+        at = pl.ds(pl.multiple_of(step * step_rows_count, step_rows_count), step_rows_count)
+        plain, turned = times_y(jnp.concatenate([main_ref[0, at, :], main_ref[1, at, :]], axis=1))
+        rows = plain - sign * turned
+        for k in range(per_step):
+            lanes = pl.ds(pl.multiple_of((first + k) * LANES, LANES), LANES)
+            pieces = [rows[(4 * k + j) * 8 : (4 * k + j + 1) * 8] for j in range(4)]
+            lower = swap_blocks([piece[:, :LANES] for piece in pieces], block_y)
+            upper = swap_blocks([piece[:, LANES:] for piece in pieces], block_y)
+            for p in range(4):
+                out_ref[group * pens + p, :, lanes] = lower[p]
+                out_ref[group * pens + 4 + p, :, lanes] = upper[p]
+        return carry
+
+    lax.fori_loop(0, groups * high_x // per_step, backward_step, 0)
+
+
+def solve_planes(incoming, me, pens, block_x, block_y):
+    import functools
+
+    angle = angles(np.arange(KY), np.arange(KY), KY)
+    y_high, y_low = table_halves(np.concatenate([np.cos(angle), np.sin(angle)], axis=1))
+    angle = angles(np.arange(KX), np.arange(KX), KX)
+    cos_x, sin_x = np.cos(angle), np.sin(angle)
+    x_high, x_low = table_halves(np.block([[cos_x, sin_x], [-sin_x, cos_x]]))
+    square_x, factor_x = np_line(KX)
+    square_y, factor_y = np_line(KY)
+    square_z, factor_z = np_line(KZ)
+    factor = jnp.asarray(np.float32(np.outer(factor_x, factor_y) / (math.pi * KX * KY * KZ)))
+    square = jnp.asarray(np.float32(square_x[:, None] + square_y[None, :]))
+    line = jnp.asarray(np.float32(np.stack([square_z, factor_z])))
+    devices, comps, lanes = incoming.shape
+    body = functools.partial(planes_body, pens=pens, block_x=block_x, block_y=block_y)
+    return pl.pallas_call(
+        body,
+        out_shape=jax.ShapeDtypeStruct((devices, comps, lanes + LANES), f32),
+        in_specs=[smem, smem] + [vmem] * 7,
+        out_specs=vmem,
+        scratch_shapes=[pltpu.VMEM((2, KX * 8, LANES), f32)] * 2,
+        name="planes",
+    )(me.reshape(1), line, incoming, y_high, y_low, x_high, x_low, factor, square)
 
 
 def modulus(index, length):
@@ -183,78 +662,42 @@
     return (potential, spectral)
 
 
-def place_tiles(spread, tiles_x, tiles_y):
-    shaped = spread.reshape(tiles_x, tiles_y, 4, 2, 4, 2, KZ)
-    total = 0.0
-    for i in range(4):
-        for j in range(4):
-            part = jnp.transpose(shaped[:, :, i, :, j], (0, 2, 1, 3, 4)).reshape(
-                2 * tiles_x, 2 * tiles_y, KZ
-            )
-            total = total + jnp.pad(part, ((2 * i, 6 - 2 * i), (2 * j, 6 - 2 * j), (0, 0)))
-    return total
-
-
-def gather_tiles(extended, tiles_x, tiles_y):
-    blocks = []
-    for i in range(4):
-        members = []
-        for j in range(4):
-            part = extended[2 * i : 2 * i + 2 * tiles_x, 2 * j : 2 * j + 2 * tiles_y]
-            part = part.reshape(tiles_x, 2, tiles_y, 2, KZ)
-            members.append(jnp.transpose(part, (0, 2, 1, 3, 4)))
-        blocks.append(jnp.stack(members, axis=3))
-    return jnp.stack(blocks, axis=2).reshape(tiles_x, tiles_y, 64, KZ)
-
-
 def local(cell_offsets, cell_z, frac, charges, tile_counts):
-    block_x = KX // lax.axis_size("grp")
-    block_y = KY // lax.axis_size("pen")
-    tiles_x = block_x // 2
+    groups_all, pens = lax.axis_size("grp"), lax.axis_size("pen")
+    devices = groups_all * pens
+    block_x = KX // groups_all
+    block_y = KY // pens
+    tiles = tile_counts.shape[0]
+    slots = charges.shape[0] // tiles
     tiles_y = block_y // 2
-    slots = charges.shape[0] // (tiles_x * tiles_y)
-    offsets = cell_offsets.reshape(2, tiles_x, tiles_y, slots)
-    zcell = cell_z.reshape(tiles_x, tiles_y, slots)
-    fracs = frac.reshape(3, tiles_x, tiles_y, slots)
-    charge = charges.reshape(tiles_x, tiles_y, slots)
-    counts = tile_counts.reshape(tiles_x, tiles_y)
-    weight_x, grade_x, weight_y, grade_y, weight_z, grade_z, live_q = tile_weights(
-        offsets, zcell, fracs, charge, counts, KZ
-    )
-    pair = weight_x[..., :, None, :] * weight_y[..., None, :, :] * live_q[..., None, None, :]
-    pair = pair.reshape(tiles_x, tiles_y, 64, slots)
-    spread = jnp.einsum("abfs,absz->abfz", pair, weight_z, precision=highest)
-    padded = place_tiles(spread, tiles_x, tiles_y)
-    rim_y = shifted(padded[: block_x + 5, block_y : block_y + 5], "pen", 1)
-    merged = padded[: block_x + 5, :block_y].at[:, :5].add(rim_y)
-    rim_x = shifted(merged[block_x : block_x + 5], "grp", 1)
-    grid = merged[:block_x].at[:5].add(rim_x)
-    potential, spectral = spectrum_pen_first(grid, block_x, block_y)
-    upper = shifted(potential[:5], "grp", -1)
-    ext_x = jnp.concatenate([potential, upper, jnp.zeros((1, block_y, KZ), jnp.float32)], axis=0)
-    beside = shifted(ext_x[:, :5], "pen", -1)
-    extended = jnp.concatenate(
-        [ext_x, beside, jnp.zeros((block_x + 6, 1, KZ), jnp.float32)], axis=1
-    )
-    footing = gather_tiles(extended, tiles_x, tiles_y)
-    main = jnp.einsum("abfz,absz->abfs", footing, weight_z, precision=highest).reshape(
-        tiles_x, tiles_y, 8, 8, slots
-    )
-    tilt = jnp.einsum("abfz,absz->abfs", footing, grade_z, precision=highest).reshape(
-        tiles_x, tiles_y, 8, 8, slots
-    )
-    force_x = -live_q * jnp.einsum(
-        "abxs,abys,abxys->abs", grade_x, weight_y, main, precision=highest
-    )
-    force_y = -live_q * jnp.einsum(
-        "abxs,abys,abxys->abs", weight_x, grade_y, main, precision=highest
-    )
-    force_z = -live_q * jnp.einsum(
-        "abxs,abys,abxys->abs", weight_x, weight_y, tilt, precision=highest
-    )
-    total = lax.psum(spectral, ("grp", "pen"))
-    forces = jnp.stack([force_x, force_y, force_z], axis=0).reshape(3, tiles_x * tiles_y * slots)
-    return (forces, total / ATOMS)
+    groups = tiles_y * slots // (2 * LANES)
+    lines = charges.shape[0] // LANES
+    offs = cell_offsets.reshape(2, lines, LANES)
+    fracs = frac.reshape(3, lines, LANES)
+    zcell = cell_z.reshape(lines, LANES)
+    charge = charges.reshape(lines, LANES)
+    sizes = (slots, groups, block_x, block_y)
+    core, rim_y, rim_x, corner = spread_charges(tile_counts, fracs, offs, zcell, charge, *sizes)
+    rims = (shifted(rim_y, "pen", 1), shifted(rim_x, "grp", 1), shifted_both(corner, 1))
+    by_planes = KZ == 8 * devices and 4 * block_y == LANES and pens == 8
+    if by_planes:
+        forward, back = z_table(devices)
+        spectral = forward_z(core, rims, *table_halves(forward)).reshape(devices, 8, block_x * block_y)
+        spectral = lax.all_to_all(spectral, ("grp", "pen"), 0, 0, tiled=True)
+        spectral = solve_planes(spectral, lax.axis_index(("grp", "pen")), pens, block_x, block_y)
+        spectral = lax.all_to_all(spectral, ("grp", "pen"), 0, 0, tiled=True)
+        core, rim_y, rim_x, corner, parts = backward_z(
+            spectral.reshape(KZ, -1), *table_halves(back.reshape(KZ, KZ)), block_x, block_y
+        )
+        total = parts[0, 0]
+    else:
+        grid = core.at[:, :8].add(rims[0]).at[:REACH].add(rims[1]).at[:REACH, :8].add(rims[2])
+        core, share = spectrum_pen_first(grid, block_x, block_y)
+        rim_y, rim_x, corner = core[:, :8], core[:REACH], core[:REACH, :8]
+        total = lax.psum(share, ("grp", "pen"))
+    rims = (shifted(rim_y, "pen", -1), shifted(rim_x, "grp", -1), shifted_both(corner, -1))
+    forces = interpolate(tile_counts, fracs, offs, zcell, charge, core, rims, *sizes)
+    return (forces.reshape(3, lines * LANES), total / (charges.shape[0] * devices))
 
 
 def solution(mesh):

time: 1150 us -> 212 us (0.18)
  local copies, waits for them, and re-layouts: 446 us -> 9.66 us
  matrix products: 265 us -> 0 us
  other arithmetic: 201 us -> 0 us
  blocking collectives: 157 us -> 58.4 us
  Pallas kernels: 0 us -> 70.1 us
    dot_general x13 -> x0, matrix products: 255 us -> none  [the longest x1 141 us: local(): spread = jnp.einsum('abfs,absz->abfz', pair, weight_z, precision=highest)]
    reshape x37 -> x0, local copies, waits for them, and re-layouts: 195 us -> none  [the longest x16 59.5 us: place_tiles(): jnp.transpose(shaped[:, :, i, :, j], (0, 2, 1, 3, 4))]
    dot_general x4 -> x0, other arithmetic: 118 us -> none  [the longest x2 60.3 us: local(): jnp.einsum('abxs,abys,abxys->abs', grade_x, weight_y, main, precision=hig...]
    transpose x19 -> x0, local copies, waits for them, and re-layouts: 97.6 us -> none  [the longest x17 86.3 us: place_tiles(): jnp.transpose(shaped[:, :, i, :, j], (0, 2, 1, 3, 4))]
    pallas_call x0 -> x5, Pallas kernels: none -> 70.1 us  [the longest x1 24.2 us: interpolate(): pl.pallas_call(body, out_shape=jax.ShapeDtypeStruct(frac.shape, f32), in_...]
    another operation x9 -> x0, local copies, waits for them, and re-layouts: 62.8 us -> none  [the longest x1 46.1 us: gather_tiles(): return jnp.stack(blocks, axis=2).reshape(tiles_x, tiles_y, 64, KZ)]
    all_to_all x3 -> x1, blocking collectives: 117 us -> 58.4 us  [local(): spectral = lax.all_to_all(spectral, ('grp', 'pen'), 0, 0, tiled=True)]
    another operation x13 -> x0, other arithmetic: 45.4 us -> none  [the longest x5 40.2 us: gather_tiles(): return jnp.stack(blocks, axis=2).reshape(tiles_x, tiles_y, 64, KZ)]
  transfers between devices with their start and end apart: 5 -> 7, of which waited for: 3 -> 6; matrix products, arithmetic and copies ran while one was open for 12% -> 1% of each run, Pallas kernels for 0% -> 0%
where the time goes in v1:
time: 212 us; the launch traced here: 208 us
  Pallas kernels  70.1 us (33%)
  blocking collectives  58.4 us (28%)
  waiting for transfers between devices  55.4 us (26%)
  starting transfers between devices  12.1 us (6%)
  local copies, waits for them, and re-layouts  9.66 us (5%)
  between operations  2.44 us (1%)
    all_to_all x1, blocking collectives, local(): spectral = lax.all_to_all(spectral, ('grp', 'pen'), 0, 0, tiled=True)  58.4 us
    all_to_all x1, waiting for transfers between devices, local(): spectral = lax.all_to_all(spectral, ('grp', 'pen'), 0, 0, tiled=True)  46.6 us
    pallas_call x1, Pallas kernels, interpolate(): pl.pallas_call(body, out_shape=jax.ShapeDtypeStruct(frac.shape, f32), in_...  24.2 us
    pallas_call x1, Pallas kernels, spread_charges(): pl.pallas_call(body, out_shape=[jax.ShapeDtypeStruct(s, f32) for s in sha...  20.4 us
    pallas_call x1, Pallas kernels, solve_planes(): pl.pallas_call(body, out_shape=jax.ShapeDtypeStruct((devices, comps, lane...  17 us
    unnamed x17, local copies, waits for them, and re-layouts  8.47 us
    ppermute x2, waiting for transfers between devices, shifted_both(): return lax.ppermute(block, ('grp', 'pen'), route)  7.6 us
    all_to_all x1, starting transfers between devices, local(): spectral = lax.all_to_all(spectral, ('grp', 'pen'), 0, 0, tiled=True)  5.14 us
  transfers between devices with their start and end apart: 7, of which 6 were waited for; matrix products, arithmetic and copies ran while one was open for 1% of the time, Pallas kernels for 0%

profile of v1, /device:TPU:8, one launch (start us, length us, event | category | flops | bytes accessed | tf_op | source)
XLA Modules:
  0.0 208.1 jit_solution(385428085547658719)
XLA Ops:
  0.6 1.7 copy.22
  2.3 1.8 copy.21
  4.1 20.4 %spread.1 = (f32[64,32,256]{2,1,0:T(8,128)}, f32[64,8,256]{2,1,0:T(8,128)}, f32[5,32,256]{2,1,0:T(8,128)}, f32[5,8,256]{2,1,0:T(8,128)}) custom-call(s32[512]{0:T(512)} %counts_ref.3, f32[3,256,128]{2,1,0:T(8,128)} %bitcast.20, s32[2,256,128]{2,1,0:T(8,128)} %bitcast.22, s32[256,128]{1,0:T(8,128)} %bitcast.25, f32[256,128]{1,0:T(8,128)} %bitcast.27), custom_call_target="tpu_custom_call" | custom-call | tf_op jit(solution)/shard_map/spread/pallas_call | solution.py:209
  24.5 0.0 collective-permute-start
  24.5 1.6 collective-permute-start.1
  26.2 2.5 %collective-permute-start.2 = (f32[5,8,256]{2,1,0:T(8,128)}, f32[5,8,256]{2,1,0:T(8,128)S(1)}, u32[]{:S(2)}, u32[]{:S(2)}) collective-permute-start(f32[5,8,256]{2,1,0:T(8,128)} %get-tuple-element.14), channel_id=1, source_target_pairs={{31,0},{24,1},{25,2},{26,3},{27,4},{28,5},{29,6},{30,7},{7,8},{0,9... | collective-permute-start | bytes 122888 | tf_op jit(solution)/shard_map/ppermute | solution.py:38
  28.6 5.2 %collective-permute-done.2.corner_ref = f32[5,8,256]{2,1,0:T(8,128)S(1)} collective-permute-done((f32[5,8,256]{2,1,0:T(8,128)}, f32[5,8,256]{2,1,0:T(8,128)S(1)}, u32[]{:S(2)}, u32[]{:S(2)}) %collective-permute-start.2) | collective-permute-done | bytes 40992 | tf_op jit(solution)/shard_map/ppermute | solution.py:38
  33.8 0.0 copy-start.6
  33.8 0.0 collective-permute-done.1.rim_x_ref
  33.8 0.0 copy-start.4
  33.8 0.9 collective-permute-done.rim_y_ref
  34.7 0.0 copy-start.2
  34.7 0.0 copy-done.6
  34.7 0.0 copy-done.4
  34.7 0.8 copy-done.2
  35.5 4.1 %forward_z.1 = f32[256,2048]{1,0:T(8,128)} custom-call(f32[64,32,256]{2,1,0:T(8,128)} %get-tuple-element.11.core_ref, f32[64,8,256]{2,1,0:T(8,128)} %copy-done.2, f32[5,32,256]{2,1,0:T(8,128)} %copy-done.4, f32[5,8,256]{2,1,0:T(8,128)} %copy-done.6, bf16[256,256]{1,0:T(8,128)(2,1)} %constant.35.high_ref, bf16[256,256]{1,0:T(8,128)(2,1)} %constant.38.low_ref), custom_call_target="tpu_custom_call" | custom-call | tf_op jit(solution)/shard_map/forward_z/pallas_call | solution.py:365
  39.6 5.1 %all-to-all-start = ((f32[32,8,2048]{2,1,0:T(8,128)}), f32[32,8,2048]{2,1,0:T(8,128)S(1)}, u32[]{:S(2)}, u32[]{:S(2)}) async-start(f32[32,8,2048]{2,1,0:T(8,128)} %bitcast.19), calls=%async_computation | async-start | bytes 4194304 | tf_op jit(solution)/shard_map/all_to_all | solution.py:686
  44.8 46.6 %all-to-all-done.in_ref = f32[32,8,2048]{2,1,0:T(8,128)S(1)} async-done(((f32[32,8,2048]{2,1,0:T(8,128)}), f32[32,8,2048]{2,1,0:T(8,128)S(1)}, u32[]{:S(2)}, u32[]{:S(2)}) %all-to-all-start) | async-done | bytes 2097184 | tf_op jit(solution)/shard_map/all_to_all | solution.py:686
  91.3 0.0 copy-start
  91.3 1.3 copy-done
  92.7 17.0 %planes.1 = f32[32,8,2176]{2,1,0:T(8,128)} custom-call(s32[1]{0:T(128)} %bitcast.2.where_ref, f32[2,256]{1,0:T(2,128)} %constant.33.clone.line_ref, f32[32,8,2048]{2,1,0:T(8,128)} %copy-done, bf16[256,512]{1,0:T(8,128)(2,1)} %constant.39.y_high_ref, bf16[256,512]{1,0:T(8,128)(2,1)} %constant.42.y_low_ref, bf16[512,512]{1,0:T(8,128)(2,1)} %constant.43.x_high_ref, ...), custom_call_target="tpu_custom_call" | custom-call | tf_op jit(solution)/shard_map/planes/pallas_call | solution.py:547
  109.7 58.4 %all_to_all.10 = f32[32,8,2176]{2,1,0:T(8,128)} all-to-all(f32[32,8,2176]{2,1,0:T(8,128)} %planes.1), channel_id=1, replica_groups=mesh['grp'=4,'pen'=8] {'grp','pen'}, dimensions={0} | all-to-all | bytes 4456448 | tf_op jit(solution)/shard_map/all_to_all | solution.py:688
  168.1 4.4 %backward_z.1 = (f32[64,32,256]{2,1,0:T(8,128)}, f32[64,8,256]{2,1,0:T(8,128)}, f32[5,32,256]{2,1,0:T(8,128)}, f32[5,8,256]{2,1,0:T(8,128)}, f32[8,128]{1,0:T(8,128)}) custom-call(f32[256,2176]{1,0:T(8,128)} %bitcast.18, bf16[256,256]{1,0:T(8,128)(2,1)} %constant.47.high_ref, bf16[256,256]{1,0:T(8,128)(2,1)} %constant.50.low_ref), custom_call_target="tpu_custom_call" | custom-call | tf_op jit(solution)/shard_map/backward_z/pallas_call | solution.py:402
  172.4 0.1 collective-permute-start.3
  172.5 1.6 collective-permute-start.4
  174.1 1.2 collective-permute-start.5
  175.3 1.2 slice.3
  177.2 2.4 %collective-permute-done.5.corner_ref = f32[5,8,256]{2,1,0:T(8,128)S(1)} collective-permute-done((f32[5,8,256]{2,1,0:T(8,128)}, f32[5,8,256]{2,1,0:T(8,128)S(1)}, u32[]{:S(2)}, u32[]{:S(2)}) %collective-permute-start.5) | collective-permute-done | bytes 40992 | tf_op jit(solution)/shard_map/ppermute | solution.py:38
  179.6 0.0 copy-start.5
  179.6 0.1 collective-permute-done.4.rim_x_ref
  179.7 0.0 copy-start.3
  179.7 0.3 collective-permute-done.3.rim_y_ref
  179.9 0.0 copy-start.1
  179.9 0.3 copy-done.5
  180.2 0.1 copy-done.3
  180.3 0.4 copy-done.1
  180.7 24.2 %interpolate.1 = f32[3,256,128]{2,1,0:T(8,128)} custom-call(s32[512]{0:T(512)} %counts_ref.3, f32[3,256,128]{2,1,0:T(8,128)} %bitcast.21, s32[2,256,128]{2,1,0:T(8,128)} %bitcast.23, s32[256,128]{1,0:T(8,128)} %bitcast.26, f32[256,128]{1,0:T(8,128)} %bitcast.28, f32[64,32,256]{2,1,0:T(8,128)} %get-tuple-element.15.core_ref, f32[64,8,256]{2,1,0:T(8,128)} %copy-done.1, ...), custom_call_target="tpu_custom_call" | custom-call | tf_op jit(solution)/shard_map/interpolate/pallas_call | solution.py:287
  204.9 2.1 copy.20
Async XLA Ops:
  24.5 10.2 %collective-permute-start = (f32[64,8,256]{2,1,0:T(8,128)}, f32[64,8,256]{2,1,0:T(8,128)S(1)}, u32[]{:S(2)}, u32[]{:S(2)}) collective-permute-start(f32[64,8,256]{2,1,0:T(8,128)} %get-tuple-element.12), channel_id=1, source_target_pairs={{7,0},{0,1},{1,2},{2,3},{3,4},{4,5},{5,6},{6,7},{15,8},{8,9},{9,10... | collective-permute-start | bytes 1572872 | tf_op jit(solution)/shard_map/ppermute | solution.py:28
  24.5 9.2 %collective-permute-start.1 = (f32[5,32,256]{2,1,0:T(8,128)}, f32[5,32,256]{2,1,0:T(8,128)S(1)}, u32[]{:S(2)}, u32[]{:S(2)}) collective-permute-start(f32[5,32,256]{2,1,0:T(8,128)} %get-tuple-element.13), channel_id=1, source_target_pairs={{24,0},{0,8},{8,16},{16,24},{25,1},{1,9},{9,17},{17,25},{26,2},{2,... | collective-permute-start | bytes 491528 | tf_op jit(solution)/shard_map/ppermute | solution.py:28
  26.2 7.6 %collective-permute-start.2 = (f32[5,8,256]{2,1,0:T(8,128)}, f32[5,8,256]{2,1,0:T(8,128)S(1)}, u32[]{:S(2)}, u32[]{:S(2)}) collective-permute-start(f32[5,8,256]{2,1,0:T(8,128)} %get-tuple-element.14), channel_id=1, source_target_pairs={{31,0},{24,1},{25,2},{26,3},{27,4},{28,5},{29,6},{30,7},{7,8},{0,9... | collective-permute-start | bytes 122888 | tf_op jit(solution)/shard_map/ppermute | solution.py:38
  33.8 0.9 copy-start.6
  33.8 0.9 copy-start.4
  34.7 0.8 copy-start.2
  39.6 51.7 %all-to-all-start = ((f32[32,8,2048]{2,1,0:T(8,128)}), f32[32,8,2048]{2,1,0:T(8,128)S(1)}, u32[]{:S(2)}, u32[]{:S(2)}) async-start(f32[32,8,2048]{2,1,0:T(8,128)} %bitcast.19), calls=%async_computation | async-start | bytes 4194304 | tf_op jit(solution)/shard_map/all_to_all | solution.py:686
  91.3 1.3 copy-start
  172.4 7.5 %collective-permute-start.3 = (f32[64,8,256]{2,1,0:T(8,128)}, f32[64,8,256]{2,1,0:T(8,128)S(1)}, u32[]{:S(2)}, u32[]{:S(2)}) collective-permute-start(f32[64,8,256]{2,1,0:T(8,128)} %get-tuple-element.16), channel_id=1, source_target_pairs={{1,0},{2,1},{3,2},{4,3},{5,4},{6,5},{7,6},{0,7},{9,8},{10,9},{11,1... | collective-permute-start | bytes 1572872 | tf_op jit(solution)/shard_map/ppermute | solution.py:28
  172.5 7.2 %collective-permute-start.4 = (f32[5,32,256]{2,1,0:T(8,128)}, f32[5,32,256]{2,1,0:T(8,128)S(1)}, u32[]{:S(2)}, u32[]{:S(2)}) collective-permute-start(f32[5,32,256]{2,1,0:T(8,128)} %get-tuple-element.17), channel_id=1, source_target_pairs={{8,0},{16,8},{24,16},{0,24},{9,1},{17,9},{25,17},{1,25},{10,2},{18... | collective-permute-start | bytes 491528 | tf_op jit(solution)/shard_map/ppermute | solution.py:28
  174.1 5.5 %collective-permute-start.5 = (f32[5,8,256]{2,1,0:T(8,128)}, f32[5,8,256]{2,1,0:T(8,128)S(1)}, u32[]{:S(2)}, u32[]{:S(2)}) collective-permute-start(f32[5,8,256]{2,1,0:T(8,128)} %get-tuple-element.18), channel_id=1, source_target_pairs={{9,0},{10,1},{11,2},{12,3},{13,4},{14,5},{15,6},{8,7},{17,8},{18,9... | collective-permute-start | bytes 122888 | tf_op jit(solution)/shard_map/ppermute | solution.py:38
  179.6 0.6 copy-start.5
  179.7 0.7 copy-start.3
  179.9 0.8 copy-start.1

commit v2 on v1

v2 whole, which is shorter than its diff:
```python
import functools
import math

import jax
import jax.numpy as jnp
import numpy as np
from jax import lax
from jax.experimental import pallas as pl
from jax.experimental.pallas import tpu as pltpu
from jax.sharding import PartitionSpec as P

KX = 256
KY = 256
KZ = 256
LANES = 128
ROWS = 16
SPAN = 7
REACH = 5

ewald_split = 0.6
highest = lax.Precision.HIGHEST
f32 = jnp.float32
bf16 = jnp.bfloat16


def shifted(block, axis, distance):
    devices = range(lax.axis_size(axis))
    route = [((i - distance) % len(devices), i) for i in devices]
    return lax.ppermute(block, axis, route)


def shifted_both(block, distance):
    groups, pens = lax.axis_size("grp"), lax.axis_size("pen")
    route = []
    for g in range(groups):
        for p in range(pens):
            source = ((g - distance) % groups) * pens + (p - distance) % pens
            route.append((source, g * pens + p))
    return lax.ppermute(block, ("grp", "pen"), route)


def halves(value):
    high = value.astype(bf16)
    low = (value - high.astype(f32)).astype(bf16)
    return high, low


def table_halves(table):
    table = jnp.asarray(np.asarray(table, np.float32))
    return halves(table)


def dot(left, right, dims):
    return lax.dot_general(left, right, (dims, ((), ())), preferred_element_type=f32)


NN = ((1,), (0,))
NT = ((1,), (1,))


def spline_rows(x):
    values = [jnp.ones_like(x)]
    fifth = None
    for order in range(2, 7):
        nxt = []
        for j in range(order):
            term = None
            if j >= 1:
                term = values[j - 1] * (x + float(order - 1 - j))
            if j <= order - 2:
                other = values[j] * (float(1 + j) - x)
                term = other if term is None else term + other
            nxt.append(term)
        if order == 5:
            fifth = [v * (1.0 / 24.0) for v in nxt]
        values = nxt
    thetas = [v * (1.0 / 120.0) for v in values]
    slopes = [-fifth[0]]
    for j in range(1, 5):
        slopes.append(fifth[j - 1] - fifth[j])
    slopes.append(fifth[4])
    return thetas, slopes


def placed(rows, offset):
    out = []
    zero = jnp.zeros_like(rows[0])
    for i in range(SPAN):
        here = rows[i] if i <= 5 else zero
        before = rows[i - 1] if i >= 1 else zero
        out.append(jnp.where(offset == 0, here, before))
    return out


def spread_out(row):
    return jnp.broadcast_to(row, (ROWS, row.shape[-1]))


def group_places(step, ranges):
    places = []
    for k in range(4):
        index = step * 4 + k
        passed = 0
        row = col = 0
        for first, last, low, high in ranges:
            width = high - low
            inside = index - passed
            a, g = first + inside // width, low + inside % width
            row, col = (a, g) if passed == 0 else (jnp.where(inside >= 0, a, row), jnp.where(inside >= 0, g, col))
            passed += (last - first) * width
        places.append((row, col))
    return places


def step_count(ranges):
    return sum((last - first) * (high - low) for first, last, low, high in ranges) // 4


def step_atoms(places, refs, slots, groups):
    counts_ref, frac_ref, offs_ref, z_ref, q_ref = refs
    per_row = LANES // slots
    lines = [(a * groups + g) * 2 + half for a, g in places for half in range(2)]

    def wide(ref, d):
        rows = [ref[d : d + 1, pl.ds(pl.multiple_of(line * LANES, LANES), LANES)] for line in lines]
        return jnp.concatenate(rows, axis=0)

    def tall(ref):
        return jnp.concatenate([ref[pl.ds(line, 1), :] for line in lines], axis=0)

    row_at = lax.broadcasted_iota(jnp.int32, (8, LANES), 0)
    lane_at = lax.broadcasted_iota(jnp.int32, (8, LANES), 1)
    tile_at = row_at * per_row + lane_at // slots
    count = jnp.zeros((8, LANES), jnp.int32)
    for r, line in enumerate(lines):
        for k in range(per_row):
            count = jnp.where(tile_at == r * per_row + k, counts_ref[line * per_row + k], count)
    charge = jnp.where(lane_at % slots < count, tall(q_ref), 0.0)
    tile_in_group = (row_at % 2) * per_row + lane_at // slots
    fracs = [wide(frac_ref, d) for d in range(3)]
    return fracs, wide(offs_ref, 0), wide(offs_ref, 1) + 2 * tile_in_group, tall(z_ref), charge, lines


def keep_rows(tab_ref, lists):
    for q, rows in enumerate(lists):
        for j, value in enumerate(rows):
            tab_ref[pl.ds(64 * q + 8 * j, 8), :] = value


def clear_rows(tab_ref):
    tab_ref[...] = jnp.zeros_like(tab_ref)


def by_distance(distance, tab_ref, q, row):
    table = tab_ref[pl.ds(64 * q + row, 8, stride=8), :]
    at = jnp.minimum(distance & 15, 7)
    return jnp.concatenate(
        [jnp.take_along_axis(table, at[k : k + 8], axis=0, mode="promise_in_bounds") for k in (0, 8)], axis=0
    )


def z_parts(zcell, row, tab_ref, lists):
    cell = spread_out(zcell[row : row + 1])
    at = lax.broadcasted_iota(jnp.int32, (ROWS, LANES), 0)
    ahead = (at - cell) & (ROWS - 1)
    block = ((cell + ahead) & (KZ - 1)) // ROWS
    weights = [by_distance(ahead, tab_ref, q, row) for q in lists]
    return block.astype(f32).astype(bf16), weights


def z_matrix(block, weight):
    zero = jnp.zeros_like(weight)
    return jnp.concatenate(
        [jnp.where(block == jnp.array(k, bf16), weight, zero) for k in range(KZ // ROWS)], axis=0
    )


def spread_body(*refs, slots, groups, ranges, base, pieces, carried):
    atom_refs = refs[:5]
    acc_ref, tab_ref = refs[-2:]
    acc_ref[...] = jnp.zeros_like(acc_ref)
    clear_rows(tab_ref)
    for piece, ref in zip(carried, refs[5:]):
        low = (piece[0] - base, piece[2])
        acc_ref[low[0] : low[0] + ref.shape[0], low[1] : low[1] + ref.shape[1]] += ref[...]
    refs = refs[5 + len(carried) :]
    at = lax.broadcasted_iota(jnp.int32, (ROWS, LANES), 0)

    def body(step, carry):
        places = group_places(step, ranges)
        fracs, offset_x, offset_y, zcell, charge, lines = step_atoms(places, atom_refs, slots, groups)
        theta_x, _ = spline_rows(fracs[0])
        theta_y, _ = spline_rows(fracs[1])
        theta_z, _ = spline_rows(fracs[2])
        theta_y = [t * charge for t in theta_y]
        weight_x = placed(theta_x, offset_x)
        keep_rows(tab_ref, [theta_z, theta_y])
        for k in range(4):
            blocks, zs, pairs = [], [], []
            for half in range(2):
                line = 2 * k + half
                row = slice(line, line + 1)
                block, (weight,) = z_parts(zcell, line, tab_ref, [0])
                blocks.append(block)
                zs.append(weight)
                weight_y = by_distance(at - spread_out(offset_y[row]), tab_ref, 1, line)
                pairs.append([spread_out(weight_x[i][row]) * weight_y for i in range(SPAN)])
            block = jnp.concatenate(blocks, axis=1)
            z_high, z_low = halves(jnp.concatenate(zs, axis=1))
            table_high = z_matrix(block, z_high)
            table_low = z_matrix(block, z_low)
            pair = jnp.concatenate(
                [jnp.concatenate([pairs[0][i], pairs[1][i]], axis=1) for i in range(SPAN)], axis=0
            )
            high, low = halves(pair)
            both = dot(jnp.concatenate([high, low], axis=0), table_high, NT)
            rest = dot(high, table_low, NT)
            total = both[: SPAN * ROWS] + both[SPAN * ROWS :] + rest
            a, g = places[k]
            where = (pl.ds(2 * a - base, SPAN), pl.ds(pl.multiple_of(8 * g, 8), ROWS))
            acc_ref[where[0], where[1], :] += total.reshape(SPAN, ROWS, KZ)
        return carry

    lax.fori_loop(0, step_count(ranges), body, 0)
    for piece, ref in zip(pieces, refs):
        ref[...] = acc_ref[piece[0] - base : piece[1] - base, piece[2] : piece[3], :]


vmem = pl.BlockSpec(memory_space=pltpu.VMEM)
room = pltpu.CompilerParams(vmem_limit_bytes=28 * 1024 * 1024)


def resident(values):
    return [pltpu.with_memory_space_constraint(value, pltpu.VMEM) for value in values]


def apart(values):
    return [pltpu.with_memory_space_constraint(value, pltpu.HBM) for value in values]


def kept(shape):
    return pltpu.VMEM(shape, f32)


def stored(shape):
    return pltpu.HBM(shape, f32)


smem = pl.BlockSpec(memory_space=pltpu.SMEM)


def spread_charges(atoms, slots, groups, block_y, ranges, pieces, holds, carried=(), fields=()):
    base = min([2 * r[0] for r in ranges] + [p[0] for p in pieces + list(carried)])
    top = max([2 * r[1] + REACH for r in ranges] + [p[1] for p in pieces + list(carried)])
    body = functools.partial(
        spread_body, slots=slots, groups=groups, ranges=ranges, base=base, pieces=pieces, carried=carried
    )
    shapes = [(p[1] - p[0], p[3] - p[2], KZ) for p in pieces]
    return pl.pallas_call(
        body,
        out_shape=[hold(s) for hold, s in zip(holds, shapes)],
        in_specs=[smem] + [vmem] * (4 + len(fields)),
        compiler_params=room,
        out_specs=[vmem] * len(shapes),
        scratch_shapes=[pltpu.VMEM((top - base, block_y + 8, KZ), f32), pltpu.VMEM((128, LANES), f32)],
        name="spread",
    )(*atoms, *fields)


def interp_body(*refs, slots, groups, ranges, base, pieces, before, first):
    atom_refs = refs[:5]
    out_ref, pot_ref, tab_ref = refs[-3:]
    clear_rows(tab_ref)
    refs = refs[5:]
    for (low_x, low_y, skip), ref in zip(pieces, refs):
        tall, wide = ref.shape[0] - skip, ref.shape[1]
        pot_ref[low_x + skip - base : low_x + skip - base + tall, low_y : low_y + wide, :] = ref[skip:]
    for k in range(before):
        earlier_ref = refs[len(pieces) + k]
        start = earlier_ref.shape[1] * k if k == 0 else out_ref.shape[1] - earlier_ref.shape[1]
        out_ref[:, start : start + earlier_ref.shape[1]] = earlier_ref[...]
    at = lax.broadcasted_iota(jnp.int32, (ROWS, LANES), 0)
    height = SPAN * ROWS

    def body(step, carry):
        places = group_places(step, ranges)
        fracs, offset_x, offset_y, zcell, charge, lines = step_atoms(places, atom_refs, slots, groups)
        theta_x, slope_x = spline_rows(fracs[0])
        theta_y, slope_y = spline_rows(fracs[1])
        theta_z, slope_z = spline_rows(fracs[2])
        theta_y = [t * -charge for t in theta_y]
        slope_y = [t * -charge for t in slope_y]
        weight_x = placed(theta_x, offset_x)
        grade_x = placed(slope_x, offset_x)
        keep_rows(tab_ref, [theta_z, slope_z, theta_y, slope_y])
        for k in range(4):
            blocks, zs, gs = [], [], []
            for half in range(2):
                block, (weight, grade) = z_parts(zcell, 2 * k + half, tab_ref, [0, 1])
                blocks.append(block)
                zs.append(weight)
                gs.append(grade)
            block = jnp.concatenate(blocks, axis=1)
            z_high, z_low = halves(jnp.concatenate(zs, axis=1))
            g_high, g_low = halves(jnp.concatenate(gs, axis=1))
            a, g = places[k]
            slab = pot_ref[pl.ds(2 * a - base, SPAN), pl.ds(pl.multiple_of(8 * g, 8), ROWS), :]
            high, low = halves(slab.reshape(height, KZ))
            stacked = jnp.concatenate([high, low], axis=0)
            main = dot(stacked, z_matrix(block, z_high), NN)
            main = main[:height] + main[height:] + dot(high, z_matrix(block, z_low), NN)
            tilt = dot(stacked, z_matrix(block, g_high), NN)
            tilt = tilt[:height] + tilt[height:] + dot(high, z_matrix(block, g_low), NN)
            for half in range(2):
                row = slice(2 * k + half, 2 * k + half + 1)
                lanes = slice(half * LANES, (half + 1) * LANES)
                away = at - spread_out(offset_y[row])
                weight_y = by_distance(away, tab_ref, 2, 2 * k + half)
                grade_y = by_distance(away, tab_ref, 3, 2 * k + half)
                plain = steep = tilted = 0.0
                for i in range(SPAN):
                    part = slice(i * ROWS, (i + 1) * ROWS)
                    wide = spread_out(weight_x[i][row])
                    plain = plain + wide * main[part, lanes]
                    tilted = tilted + wide * tilt[part, lanes]
                    steep = steep + spread_out(grade_x[i][row]) * main[part, lanes]
                forces = [
                    jnp.sum(steep * weight_y, axis=0, keepdims=True),
                    jnp.sum(plain * grade_y, axis=0, keepdims=True),
                    jnp.sum(tilted * weight_y, axis=0, keepdims=True),
                ]
                start = (lines[2 * k + half] - first) * LANES
                out_ref[:, pl.ds(pl.multiple_of(start, LANES), LANES)] = jnp.concatenate(forces, axis=0)
        return carry

    lax.fori_loop(0, step_count(ranges), body, 0)


def interpolate(atoms, slots, groups, block_y, ranges, pieces, fields, rows, hold, earlier=()):
    base = min(2 * r[0] for r in ranges)
    line = 2 * groups
    body = functools.partial(
        interp_body, slots=slots, groups=groups, ranges=ranges, base=base, pieces=pieces,
        before=len(earlier), first=rows[0] * line,
    )
    height = max(max(2 * r[1] + REACH for r in ranges), max(p[0] + f.shape[0] for p, f in zip(pieces, fields))) - base
    return pl.pallas_call(
        body,
        out_shape=hold((3, (rows[1] - rows[0]) * line * LANES)),
        in_specs=[smem] + [vmem] * (4 + len(fields) + len(earlier)),
        compiler_params=room,
        out_specs=vmem,
        scratch_shapes=[pltpu.VMEM((height, block_y + 8, KZ), f32), pltpu.VMEM((256, LANES), f32)],
        name="interpolate",
    )(*atoms, *fields, *earlier)


def angles(left, right, length):
    return (np.outer(left, right) % length) * (2.0 * math.pi / length)


def np_modulus(length):
    index = np.arange(length)
    coeffs = (1.0 / 120.0, 26.0 / 120.0, 66.0 / 120.0, 26.0 / 120.0, 1.0 / 120.0)
    total = 0.0
    for j in range(5):
        total = total + coeffs[j] * np.exp(2j * math.pi * ((index * j) % length) / length)
    return np.abs(total) ** 2


def np_line(length):
    index = np.arange(length)
    freq = np.where(2 * index < length, index, index - length) / length
    square = freq * freq
    return square, np.exp(-(math.pi**2) * square / ewald_split**2) / np_modulus(length)


def z_table(devices):
    per = KZ // 2 // devices
    position = np.arange(KZ)
    forward, back = [], []
    for device in range(devices):
        for imaginary in range(2):
            for plane in range(device * per, (device + 1) * per):
                wave = 2.0 * math.pi * ((plane * position) % KZ) / KZ
                if plane == 0:
                    row = np.where(position % 2 == 0, 1.0, -1.0) if imaginary else np.ones(KZ)
                    forward.append(row)
                    back.append(row)
                else:
                    row = -np.sin(wave) if imaginary else np.cos(wave)
                    forward.append(row)
                    back.append(2.0 * row)
    return np.stack(forward), np.stack(back)


def forward_z_body(core_ref, rim_y_ref, *refs, chunk, first):
    out_ref = refs[-1]
    high = refs[-3][...]
    low = refs[-2][...]
    sides = refs[:-3]
    block_x, block_y = core_ref.shape[:2]
    stacked = jnp.concatenate([high, low], axis=0)
    size = high.shape[0]
    for start in range(0, block_x, chunk):
        part = core_ref[start : start + chunk]
        edge = part[:, :8] + rim_y_ref[first + start : first + start + chunk]
        rest = part[:, 8:]
        if sides and start < REACH:
            count = min(REACH - start, chunk)
            side = sides[0][start : start + count]
            fix = side[:, :8] + sides[1][start : start + count]
            edge = jnp.concatenate([edge[:count] + fix, edge[count:]], axis=0)
            rest = jnp.concatenate([rest[:count] + side[:, 8:], rest[count:]], axis=0)
        part = jnp.concatenate([edge, rest], axis=1).reshape(chunk * block_y, KZ)
        part_high, part_low = halves(part)
        both = dot(stacked, part_high, NT)
        total = both[:size] + both[size:] + dot(high, part_low, NT)
        out_ref[:, start * block_y : (start + chunk) * block_y] = total


def forward_z(core, rims, high, low, first):
    block_x, block_y = core.shape[:2]
    chunk = 256 // block_y
    return pl.pallas_call(
        functools.partial(forward_z_body, chunk=chunk, first=first),
        out_shape=kept((KZ, block_x * block_y)),
        in_specs=[vmem] * (3 + len(rims)),
        compiler_params=room,
        out_specs=vmem,
        name="forward_z",
    )(*resident([core, *rims]), high, low)


def backward_z_body(in_ref, high_ref, low_ref, core_ref, rim_y_ref, *refs, chunk, scale):
    block_x, block_y = core_ref.shape[:2]
    high = high_ref[...]
    low = low_ref[...]
    for start in range(0, block_x, chunk):
        part = in_ref[:, start * block_y : (start + chunk) * block_y].T
        part_high, part_low = halves(part)
        size = part.shape[0]
        both = dot(jnp.concatenate([part_high, part_low], axis=0), high, NN)
        total = both[:size] + both[size:] + dot(part_high, low, NN)
        total = total.reshape(chunk, block_y, KZ)
        core_ref[start : start + chunk] = total
        rim_y_ref[start : start + chunk] = total[:, :8]
        if len(refs) == 3:
            if start < REACH:
                count = min(REACH - start, chunk)
                refs[0][start : start + count] = total[:count]
                refs[1][start : start + count] = total[:count, :8]
            over = block_x - refs[2].shape[0]
            if start >= over:
                refs[2][start - over : start - over + chunk] = total
    if len(refs) == 1:
        tail = in_ref[:, block_x * block_y :]
        refs[0][0] = jnp.max(jnp.sum(tail.reshape(-1, 8, LANES), axis=0)) * scale


def backward_z(spectral, high, low, block_x, block_y, others, scale=None):
    chunk = 256 // block_y
    sent = [(block_x, 8, KZ)] + others
    total = [] if scale is None else [jax.ShapeDtypeStruct((1,), f32)]
    return pl.pallas_call(
        functools.partial(backward_z_body, chunk=chunk, scale=scale),
        out_shape=[kept((block_x, block_y, KZ))] + [stored(s) for s in sent] + total,
        in_specs=[vmem] * 3,
        compiler_params=room,
        out_specs=[vmem] * (1 + len(sent)) + [smem] * len(total),
        name="backward_z",
    )(*resident([spectral]), *apart([high, low]))


def swap_blocks(parts, width):
    lane_at = lax.broadcasted_iota(jnp.int32, parts[0].shape, 1)
    first = lane_at < 2 * width
    even = (lane_at // width) % 2 == 0
    a, b, c, d = parts
    a, c = jnp.where(first, a, pltpu.roll(c, 2 * width, 1)), jnp.where(first, pltpu.roll(a, 2 * width, 1), c)
    b, d = jnp.where(first, b, pltpu.roll(d, 2 * width, 1)), jnp.where(first, pltpu.roll(b, 2 * width, 1), d)
    back = LANES - width
    a, b = jnp.where(even, a, pltpu.roll(b, width, 1)), jnp.where(even, pltpu.roll(a, back, 1), b)
    c, d = jnp.where(even, c, pltpu.roll(d, width, 1)), jnp.where(even, pltpu.roll(c, back, 1), d)
    return [a, b, c, d]


STEP = 256


def times_y(rows, y_high, y_low):
    high, low = halves(rows)
    size = rows.shape[0]
    both = dot(jnp.concatenate([high, low], axis=0), y_high, NN)
    total = both[:size] + both[size:] + dot(high, y_low, NN)
    turned = pltpu.roll(total[:, KY:].reshape(size // 8, 8, KY), 4, 1).reshape(size, KY)
    return total[:, :KY], turned


def row_sign():
    comp_at = lax.broadcasted_iota(jnp.int32, (STEP, KY), 0) % 8
    return jnp.where(comp_at < 4, 1.0, -1.0)


def forward_y(in_ref, y_high_ref, y_low_ref, main_ref, twin_ref, pens, width):
    y_high = y_high_ref[...]
    y_low = y_low_ref[...]
    sign = row_sign()
    per_step = STEP // 32
    spans = in_ref.shape[2] // LANES // per_step
    groups = in_ref.shape[0] // pens

    def body(step, carry):
        group = step // spans
        rows = []
        for k in range(per_step):
            at = (step % spans) * per_step + k
            lanes = pl.ds(pl.multiple_of(at * LANES, LANES), LANES)
            lower = swap_blocks([in_ref[group * pens + p, :, lanes] for p in range(4)], width)
            upper = swap_blocks([in_ref[group * pens + 4 + p, :, lanes] for p in range(4)], width)
            for low, up in zip(lower, upper):
                rows.append(jnp.concatenate([low, up], axis=1))
        plain, turned = times_y(jnp.concatenate(rows, axis=0), y_high, y_low)
        at = pl.ds(pl.multiple_of(step * STEP, STEP), STEP)
        main = plain + sign * turned
        twin = sign * plain - turned
        for k in range(2):
            side = slice(k * LANES, (k + 1) * LANES)
            main_ref[k, at, :] = main[:, side]
            twin_ref[k, at, :] = twin[:, side]
        return carry

    lax.fori_loop(0, groups * spans, body, 0)


def backward_y(main_ref, y_high_ref, y_low_ref, out_ref, pens, width, lines):
    y_high = y_high_ref[...]
    y_low = y_low_ref[...]
    sign = row_sign()
    per_step = STEP // 32
    spans = lines // LANES // per_step
    groups = out_ref.shape[0] // pens

    def body(step, carry):
        group = step // spans
        at = pl.ds(pl.multiple_of(step * STEP, STEP), STEP)
        joined = jnp.concatenate([main_ref[0, at, :], main_ref[1, at, :]], axis=1)
        plain, turned = times_y(joined, y_high, y_low)
        rows = plain - sign * turned
        for k in range(per_step):
            at = (step % spans) * per_step + k
            lanes = pl.ds(pl.multiple_of(at * LANES, LANES), LANES)
            pieces = [rows[(4 * k + j) * 8 : (4 * k + j + 1) * 8] for j in range(4)]
            lower = swap_blocks([piece[:, :LANES] for piece in pieces], width)
            upper = swap_blocks([piece[:, LANES:] for piece in pieces], width)
            for p in range(4):
                out_ref[group * pens + p, :, lanes] = lower[p]
                out_ref[group * pens + 4 + p, :, lanes] = upper[p]
        return carry

    lax.fori_loop(0, groups * spans, body, 0)


def planes_first_body(in_ref, y_high_ref, y_low_ref, main_ref, twin_ref, *, pens, width):
    forward_y(in_ref, y_high_ref, y_low_ref, main_ref, twin_ref, pens, width)


def planes_last_body(main_ref, energy_ref, y_high_ref, y_low_ref, out_ref, *, pens, width, lines):
    backward_y(main_ref, y_high_ref, y_low_ref, out_ref, pens, width, lines)
    out_ref[:, :, lines:] = jnp.broadcast_to(energy_ref[...].reshape(1, 8, LANES), (out_ref.shape[0], 8, LANES))


def planes_body(
    where_ref, line_ref, in_ref, far_ref, far_twin_ref, y_high_ref, y_low_ref, x_high_ref, x_low_ref,
    column_ref, row_ref, out_ref, far_out_ref, energy_ref, main_ref, twin_ref,
    *, pens, width,
):
    me = where_ref[0]
    forward_y(in_ref, y_high_ref, y_low_ref, main_ref, twin_ref, pens, width)
    near = main_ref.shape[1] // 8

    def times_x(real, imag):
        high, low = [
            jnp.concatenate(
                [jnp.concatenate([r, i], axis=1), jnp.concatenate([i, -r], axis=1)], axis=0
            )
            for r, i in zip(halves(real), halves(imag))
        ]
        x_high = x_high_ref[...]
        total = dot(x_high, high, NN) + dot(x_high, low, NN) + dot(x_low_ref[...], high, NN)
        return total[:, :KY], total[:, KY:]

    def plane_of(near_ref, far_ref, comp):
        def whole(ref):
            return jnp.concatenate([ref[k, pl.ds(comp, ref.shape[1] // 8, stride=8), :] for k in range(2)], axis=1)

        return jnp.concatenate([whole(near_ref), whole(far_ref)], axis=0)

    def influence(entry):
        square = column_ref[0] + (row_ref[0] + line_ref[0, entry])
        value = column_ref[1] * (row_ref[1] * line_ref[1, entry]) / jnp.where(square > 0, square, 1.0)
        return jnp.where(square > 0, value, 0.0)

    energy = jnp.zeros((KX, KY), f32)
    for plane in range(4):
        real, imag = times_x(plane_of(main_ref, far_ref, plane), plane_of(main_ref, far_ref, plane + 4))
        kernel = influence(me * 4 + plane)
        if plane == 0:
            mine = me == 0
            other = influence(KZ // 2)
            share = jnp.where(mine, 0.5 * (kernel + other), kernel)
            cross = jnp.where(mine, 0.5 * (kernel - other), 0.0)
            twin_real, twin_imag = times_x(
                plane_of(twin_ref, far_twin_ref, 0), plane_of(twin_ref, far_twin_ref, 4)
            )
            out_real = share * real + cross * twin_real
            out_imag = share * imag + cross * twin_imag
            energy = energy + jnp.where(mine, 0.5, 1.0) * (real * out_real + imag * out_imag)
        else:
            out_real = kernel * real
            out_imag = kernel * imag
            energy = energy + (real * out_real + imag * out_imag)
        real, imag = times_x(out_real, -out_imag)
        for k in range(2):
            side = slice(k * LANES, (k + 1) * LANES)
            main_ref[k, pl.ds(plane, near, stride=8), :] = real[:near, side]
            main_ref[k, pl.ds(plane + 4, near, stride=8), :] = -imag[:near, side]
            far_out_ref[k, pl.ds(plane, KX - near, stride=8), :] = real[near:, side]
            far_out_ref[k, pl.ds(plane + 4, KX - near, stride=8), :] = -imag[near:, side]

    total = jnp.sum(jnp.sum(energy, axis=0, keepdims=True), axis=1, keepdims=True)
    energy_ref[...] = jnp.broadcast_to(total, (8, LANES))
    backward_y(main_ref, y_high_ref, y_low_ref, out_ref, pens, width, out_ref.shape[2])


def plane_tables(block_x):
    angle = angles(np.arange(KY), np.arange(KY), KY)
    tables_y = table_halves(np.concatenate([np.cos(angle), np.sin(angle)], axis=1))
    order = np.arange(KX).reshape(KX // block_x, 2, block_x // 2).transpose(1, 0, 2).reshape(-1)
    angle = angles(order, order, KX)
    cos_x, sin_x = np.cos(angle), np.sin(angle)
    tables_x = table_halves(np.concatenate([cos_x, sin_x], axis=1))
    square_x, factor_x = np_line(KX)
    square_y, factor_y = np_line(KY)
    square_z, factor_z = np_line(KZ)
    factor_z = factor_z / (math.pi * KX * KY * KZ)
    column = jnp.asarray(np.float32(np.stack([square_x[order], factor_x[order]])))[:, :, None]
    row = jnp.asarray(np.float32(np.stack([square_y, factor_y])))[:, None, :]
    line = jnp.asarray(np.float32(np.stack([square_z, factor_z])))
    return tables_y, tables_x, column, row, line


def by_halves(atoms, slots, groups, block_x, block_y):
    groups_all, pens = lax.axis_size("grp"), lax.axis_size("pen")
    devices = groups_all * pens
    half = block_x // 2
    lines = half * block_y
    cut = (half - SPAN) // 2
    tiles_x = block_x // 2
    late = tiles_x - 4
    inner = groups - 1
    forward, back = z_table(devices)
    forward, back = table_halves(forward), table_halves(back.reshape(KZ, KZ))
    tables_y, tables_x, column, row, line = plane_tables(block_x)
    me = lax.axis_index(("grp", "pen")).reshape(1)
    sizes = (slots, groups, block_y)
    axes = ("grp", "pen")
    def exchange(spectral):
        return lax.all_to_all(spectral.reshape(devices, 8, -1), axes, 0, 0, tiled=True)

    edge_y = 8 * inner
    rim_pieces = [
        (0, block_x, block_y, block_y + 8),
        (block_x, block_x + REACH, 0, block_y), (block_x, block_x + REACH, block_y, block_y + 8),
    ]
    carried = [(0, half, edge_y, block_y), (half, block_x, edge_y, block_y), (2 * late, block_x, 0, edge_y)]
    ranges = [(0, tiles_x, inner, groups), (late, tiles_x, 0, inner)]
    rim_y, rim_x, corner, near_edge, far_edge, end = spread_charges(
        atoms, *sizes, ranges, rim_pieces + carried, [stored] * 4 + [kept] * 2
    )
    rim_y = shifted(rim_y, "pen", 1)
    rim_x = shifted(rim_x, "grp", 1)
    corner = shifted_both(corner, 1)
    pieces = [(half, block_x, 0, block_y), (2 * cut, half, 0, block_y)]
    atoms = [atoms[0], *resident(atoms[1:3]), *atoms[3:]]
    core, over = spread_charges(
        atoms, *sizes, [(cut, late, 0, inner)], pieces, [kept, stored], carried[1:], resident([far_edge, end])
    )
    far = forward_z(core, (rim_y,), *forward, half)
    over, far, rim_x, corner = lax.optimization_barrier((over, far, rim_x, corner))
    far = exchange(far)
    core, = spread_charges(
        atoms, *sizes, [(0, cut, 0, inner)], [(0, half, 0, block_y)], [kept],
        [pieces[1], (0, half, edge_y, block_y)], apart([over, near_edge]),
    )
    near = exchange(forward_z(core, (rim_y, rim_x, corner), *forward, 0))

    part = stored((2, KX // 2 * 8, LANES))
    far, far_twin = pl.pallas_call(
        functools.partial(planes_first_body, pens=pens, width=block_y),
        out_shape=[part, part],
        in_specs=[vmem] * 3,
        compiler_params=room,
        out_specs=[vmem] * 2,
        name="planes_first",
    )(*resident([far]), *apart(tables_y))
    near, far, energy = pl.pallas_call(
        functools.partial(planes_body, pens=pens, width=block_y),
        out_shape=[
            kept((devices, 8, lines)), part, stored((8, LANES)),
        ],
        in_specs=[smem, smem] + [vmem] * 9,
        compiler_params=room,
        out_specs=[vmem] * 3,
        scratch_shapes=[pltpu.VMEM(part.shape, f32)] * 2,
        name="planes",
    )(me, *apart([line]), *resident([near]), *apart([far, far_twin, *tables_y, *tables_x, column, row]))
    near = exchange(near)
    far = pl.pallas_call(
        functools.partial(planes_last_body, pens=pens, width=block_y, lines=lines),
        out_shape=kept((devices, 8, lines + LANES)),
        in_specs=[vmem] * 4,
        compiler_params=room,
        out_specs=vmem,
        name="planes_last",
    )(*apart([far, energy, *tables_y]))
    far = exchange(far)
    edges = [(REACH, block_y, KZ), (REACH, 8, KZ), (half - 2 * cut, block_y, KZ)]
    near, near_y, rim_x, corner, over = backward_z(near.reshape(KZ, -1), *back, half, block_y, edges)
    near_y = shifted(near_y, "pen", -1)
    rim_x = shifted(rim_x, "grp", -1)
    corner = shifted_both(corner, -1)
    pieces = [(0, 0, 0), (0, block_y, 0)]
    first = interpolate(
        atoms, *sizes, [(0, cut, 0, groups)], pieces, resident([near, near_y]), (0, cut), stored
    )
    far, first, rim_x, corner = lax.optimization_barrier((far, first, rim_x, corner))
    far, far_y, parts = backward_z(far.reshape(KZ, -1), *back, half, block_y, [], 1.0 / (devices * atoms[3].size))
    moved_y = shifted(far_y, "pen", -1)
    pieces = [(2 * cut, 0, 0), (half, 0, 0), (block_x, 0, 0)]
    over, = apart([over])
    far, rim_x, corner, near_y = resident([far, rim_x, corner, near_y])
    fields = (over, far, rim_x)
    second = interpolate(
        atoms, *sizes, [(cut, tiles_x, 0, inner)], pieces, fields, (cut, tiles_x), kept
    )
    pieces += [(0, block_y, 2 * cut), (half, block_y, 0), (block_x, block_y, 0)]
    fields += (near_y, *resident([moved_y]), corner)
    forces = interpolate(
        atoms, *sizes, [(cut, tiles_x, inner, groups)], pieces, fields, (0, tiles_x), stored,
        (*apart([first]), *resident([second])),
    )
    return forces, parts.reshape(())


def by_pencils(atoms, slots, groups, block_x, block_y):
    sizes = (slots, groups, block_y)
    ranges = [(0, block_x // 2, 0, groups)]
    pieces = [
        (0, block_x, 0, block_y), (0, block_x, block_y, block_y + 8),
        (block_x, block_x + REACH, 0, block_y), (block_x, block_x + REACH, block_y, block_y + 8),
    ]
    core, rim_y, rim_x, corner = spread_charges(atoms, *sizes, ranges, pieces, [stored] * 4)
    rims = (shifted(rim_y, "pen", 1), shifted(rim_x, "grp", 1), shifted_both(corner, 1))
    grid = core.at[:, :8].add(rims[0]).at[:REACH].add(rims[1]).at[:REACH, :8].add(rims[2])
    core, share = spectrum_pen_first(grid, block_x, block_y)
    rims = (shifted(core[:, :8], "pen", -1), shifted(core[:REACH], "grp", -1), shifted_both(core[:REACH, :8], -1))
    pieces = [(0, 0, 0), (0, block_y, 0), (block_x, 0, 0), (block_x, block_y, 0)]
    forces = interpolate(atoms, *sizes, ranges, pieces, (core, *rims), (0, block_x // 2), stored)
    total = lax.psum(share, ("grp", "pen"))
    return forces, total / (atoms[3].size * lax.axis_size("grp") * lax.axis_size("pen"))


def modulus(index, length):
    coeffs = (1.0 / 120.0, 26.0 / 120.0, 66.0 / 120.0, 26.0 / 120.0, 1.0 / 120.0)
    real_part = 0.0
    imag_part = 0.0
    for j in range(5):
        angle = (index * j % length).astype(jnp.float32) * (2.0 * math.pi / length)
        real_part = real_part + coeffs[j] * jnp.cos(angle)
        imag_part = imag_part + coeffs[j] * jnp.sin(angle)
    return real_part * real_part + imag_part * imag_part


def influence(index_x, index_y, index_z):
    freq_x = jnp.where(2 * index_x < KX, index_x, index_x - KX).astype(jnp.float32) / KX
    freq_y = jnp.where(2 * index_y < KY, index_y, index_y - KY).astype(jnp.float32) / KY
    freq_z = jnp.where(2 * index_z < KZ, index_z, index_z - KZ).astype(jnp.float32) / KZ
    square = freq_x * freq_x + freq_y * freq_y + freq_z * freq_z
    safe = jnp.where(square > 0, square, 1.0)
    volume = float(KX * KY * KZ)
    value = jnp.exp(-math.pi**2 * safe / ewald_split**2) / (math.pi * volume * safe)
    value = value / (modulus(index_x, KX) * modulus(index_y, KY) * modulus(index_z, KZ))
    return jnp.where(square > 0, value, 0.0)


def dft_tables(length):
    index = jnp.arange(length, dtype=jnp.int32)
    angle = (index[:, None] * index[None, :] % length).astype(jnp.float32) * (
        2.0 * math.pi / length
    )
    return (jnp.cos(angle), jnp.sin(angle))


def z_slots(groups):
    planes = KZ // (2 * groups) + 1
    owner = jnp.arange(groups, dtype=jnp.int32)[:, None]
    within = jnp.arange(planes, dtype=jnp.int32)[None, :]
    ordinary = owner * (planes - 1) + within
    frequency = jnp.where(within < planes - 1, ordinary, jnp.where(owner == 0, KZ // 2, 0))
    plane_weight = jnp.where(
        within < planes - 1, jnp.where(frequency == 0, 1.0, 2.0), jnp.where(owner == 0, 1.0, 0.0)
    )
    frequency = frequency.reshape(-1)
    plane_weight = plane_weight.reshape(-1).astype(jnp.float32)
    position = jnp.arange(KZ, dtype=jnp.int32)
    angle = (frequency[:, None] * position[None, :] % KZ).astype(jnp.float32) * (2.0 * math.pi / KZ)
    usable = (plane_weight > 0).astype(jnp.float32)[:, None]
    return (planes, frequency, plane_weight, jnp.cos(angle) * usable, jnp.sin(angle) * usable)


def forward_complex(data, cos_table, sin_table, shape, axis):
    direct = jnp.dot(cos_table, data, precision=highest).reshape(shape)
    other = jnp.dot(sin_table, data, precision=highest).reshape(shape)
    real_part = jnp.take(direct, 0, axis=axis) + jnp.take(other, 1, axis=axis)
    imag_part = jnp.take(direct, 1, axis=axis) - jnp.take(other, 0, axis=axis)
    return (real_part, imag_part)


def inverse_complex(data, cos_table, sin_table, shape, axis):
    direct = jnp.dot(cos_table, data, precision=highest).reshape(shape)
    other = jnp.dot(sin_table, data, precision=highest).reshape(shape)
    real_part = jnp.take(direct, 0, axis=axis) - jnp.take(other, 1, axis=axis)
    imag_part = jnp.take(other, 0, axis=axis) + jnp.take(direct, 1, axis=axis)
    return (real_part, imag_part)


def spectrum_pen_first(grid, block_x, block_y):
    cos_x, sin_x = dft_tables(KX)
    cos_y, sin_y = dft_tables(KY)
    planes, frequency, plane_weight, cos_z, sin_z = z_slots(lax.axis_size("pen"))
    slot_total = cos_z.shape[0]
    lines = KY // lax.axis_size("grp")
    real_z = jnp.einsum("xyz,kz->ykx", grid, cos_z, precision=highest)
    imag_z = -jnp.einsum("xyz,kz->ykx", grid, sin_z, precision=highest)
    outgoing = jnp.stack([real_z, imag_z], axis=2).reshape(block_y, slot_total * 2 * block_x)
    columns = lax.all_to_all(outgoing, "pen", split_axis=1, concat_axis=0, tiled=True)
    real_y, imag_y = forward_complex(columns, cos_y, sin_y, (KY, planes, 2, block_x), 2)
    sectioned = jnp.transpose(jnp.stack([real_y, imag_y], axis=-1), (2, 0, 1, 3)).reshape(
        block_x, KY * planes * 2
    )
    rows = lax.all_to_all(sectioned, "grp", split_axis=1, concat_axis=0, tiled=True)
    real_x, imag_x = forward_complex(rows, cos_x, sin_x, (KX, lines, planes, 2), 3)
    first = lax.axis_index("pen") * planes
    index_x = jnp.arange(KX, dtype=jnp.int32)[:, None, None]
    index_y = lax.axis_index("grp") * lines + jnp.arange(lines, dtype=jnp.int32)[None, :, None]
    index_z = lax.dynamic_slice_in_dim(frequency, first, planes)[None, None, :]
    local_weight = lax.dynamic_slice_in_dim(plane_weight, first, planes)[None, None, :]
    kernel = influence(index_x, index_y, index_z)
    spectral = 0.5 * jnp.sum(local_weight * kernel * (real_x * real_x + imag_x * imag_x))
    scaled = jnp.stack([kernel * real_x, kernel * imag_x], axis=-1).reshape(KX, lines * planes * 2)
    real_b, imag_b = inverse_complex(scaled, cos_x, sin_x, (KX, lines, planes, 2), 3)
    returning = jnp.stack([real_b, imag_b], axis=-1).reshape(KX, lines * planes * 2)
    rows_home = lax.all_to_all(returning, "grp", split_axis=0, concat_axis=1, tiled=True)
    rows_home = jnp.transpose(rows_home.reshape(block_x, KY, planes, 2), (1, 2, 3, 0)).reshape(
        KY, planes * 2 * block_x
    )
    real_c, imag_c = inverse_complex(rows_home, cos_y, sin_y, (KY, planes, 2, block_x), 2)
    leaving = jnp.stack([real_c, imag_c], axis=2).reshape(KY, planes * 2 * block_x)
    home = lax.all_to_all(leaving, "pen", split_axis=0, concat_axis=1, tiled=True).reshape(
        block_y, slot_total, 2, block_x
    )
    potential = jnp.einsum(
        "ykx,kz->xyz", home[:, :, 0], plane_weight[:, None] * cos_z, precision=highest
    )
    potential = potential - jnp.einsum(
        "ykx,kz->xyz", home[:, :, 1], plane_weight[:, None] * sin_z, precision=highest
    )
    return (potential, spectral)


def local(cell_offsets, cell_z, frac, charges, tile_counts):
    groups_all, pens = lax.axis_size("grp"), lax.axis_size("pen")
    devices = groups_all * pens
    block_x = KX // groups_all
    block_y = KY // pens
    slots = charges.shape[0] // tile_counts.shape[0]
    groups = block_y // 2 * slots // (2 * LANES)
    lines = charges.shape[0] // LANES
    slot_arrays = [frac, cell_offsets, cell_z.reshape(lines, LANES), charges.reshape(lines, LANES)]
    atoms = apart([tile_counts, *slot_arrays])
    if KZ == 8 * devices and 4 * block_y == LANES and pens == 8 and block_x % 16 == 0:
        return by_halves(atoms, slots, groups, block_x, block_y)
    return by_pencils(atoms, slots, groups, block_x, block_y)


def solution(mesh):
    in_specs = (
        P(None, ("grp", "pen")),
        P(("grp", "pen")),
        P(None, ("grp", "pen")),
        P(("grp", "pen")),
        P(("grp", "pen")),
    )
    out_specs = (P(None, ("grp", "pen")), P())
    return jax.shard_map(local, mesh=mesh, in_specs=in_specs, out_specs=out_specs, check_vma=False)
```

time: 212 us -> 182 us (0.86); the launches traced: 208 us -> 182 us
  blocking collectives: 58.4 us -> 0 us
  waiting for transfers between devices: 55.4 us -> 72.9 us
  starting transfers between devices: 12.1 us -> 29.3 us
  local copies, waits for them, and re-layouts: 9.66 us -> 0.02 us
  Pallas kernels: 70.1 us -> 78.6 us
    all_to_all x1 -> x0, blocking collectives: 58.4 us -> none  [local(): spectral = lax.all_to_all(spectral, ('grp', 'pen'), 0, 0, tiled=True)]
    all_to_all x1 -> x4, waiting for transfers between devices: 46.6 us -> 59 us  [exchange(): lax.all_to_all(spectral.reshape(devices, 8, -1), axes, 0, 0, tiled=True)]
    all_to_all x1 -> x4, starting transfers between devices: 5.14 us -> 17.4 us  [exchange(): lax.all_to_all(spectral.reshape(devices, 8, -1), axes, 0, 0, tiled=True)]
    pallas_call x5 -> x13, Pallas kernels: 70.1 us -> 78.6 us  [the longest x3 26.4 us: interpolate(): pl.pallas_call(body, out_shape=hold((3, (rows[1] - rows[0]) * line * LANE...]
    unnamed x17 -> x8, local copies, waits for them, and re-layouts: 8.47 us -> 0.02 us
    ppermute x2, waiting for transfers between devices: 7.6 us -> 11.1 us  [shifted_both(): return lax.ppermute(block, ('grp', 'pen'), route)]
    ppermute x4 -> x5, starting transfers between devices: 3.31 us -> 6.5 us  [shifted(): return lax.ppermute(block, axis, route)]
  transfers between devices with their start and end apart: 7 -> 11, of which waited for: 6 -> 6; matrix products, arithmetic and copies ran while one was open for 1% -> 0% of each run, Pallas kernels for 0% -> 28%
where the time goes in v2:
time: 182 us
  Pallas kernels  78.6 us (43%)
  waiting for transfers between devices  72.9 us (40%)
  starting transfers between devices  29.3 us (16%)
    all_to_all x4, waiting for transfers between devices, exchange(): lax.all_to_all(spectral.reshape(devices, 8, -1), axes, 0, 0, tiled=True)  59 us
    pallas_call x3, Pallas kernels, interpolate(): pl.pallas_call(body, out_shape=hold((3, (rows[1] - rows[0]) * line * LANE...  26.4 us
    pallas_call x3, Pallas kernels, spread_charges(): pl.pallas_call(body, out_shape=[hold(s) for hold, s in zip(holds, shapes)...  23.1 us
    all_to_all x4, starting transfers between devices, exchange(): lax.all_to_all(spectral.reshape(devices, 8, -1), axes, 0, 0, tiled=True)  17.4 us
    pallas_call x1, Pallas kernels, by_halves(): pl.pallas_call(functools.partial(planes_body, pens=pens, width=block_y),...  12 us
    ppermute x2, waiting for transfers between devices, shifted_both(): return lax.ppermute(block, ('grp', 'pen'), route)  11.1 us
    ppermute x5, starting transfers between devices, shifted(): return lax.ppermute(block, axis, route)  6.5 us
    ppermute x2, starting transfers between devices, shifted_both(): return lax.ppermute(block, ('grp', 'pen'), route)  5.43 us
  transfers between devices with their start and end apart: 11, of which 6 were waited for; matrix products, arithmetic and copies ran while one was open for 0% of the time, Pallas kernels for 28%

profile of v2, /device:TPU:8, one launch (start us, length us, event | category | flops | bytes accessed | tf_op | source)
XLA Modules:
  0.0 181.5 jit_solution(6113205894313323034)
XLA Ops:
  0.6 0.0 copy-start
  0.6 0.0 copy-start.1
  0.6 0.0 copy-start.2
  0.7 0.0 copy-start.3
  0.7 8.5 %spread.3 = (f32[64,8,256]{2,1,0:T(8,128)}, f32[5,32,256]{2,1,0:T(8,128)}, f32[5,8,256]{2,1,0:T(8,128)}, f32[32,8,256]{2,1,0:T(8,128)}, f32[32,8,256]{2,1,0:T(8,128)S(1)}, /*index=5*/f32[8,24,256]{2,1,0:T(8,128)S(1)}) custom-call(s32[512]{0:T(512)} %refs_0_.11, f32[3,32768]{1,0:T(4,128)} %refs_1_.11, s32[2,32768]{1,0:T(2,128)} %refs_2_.11, ...), custom_call_target="tpu_custom_call" | custom-call | tf_op jit(solution)/shard_map/spread/pallas_call | solution.py:259
  9.1 0.0 collective-permute-start
  9.1 1.6 collective-permute-start.1
  10.7 2.5 %collective-permute-start.2 = (f32[5,8,256]{2,1,0:T(8,128)}, f32[5,8,256]{2,1,0:T(8,128)S(1)}, u32[]{:S(2)}, u32[]{:S(2)}) collective-permute-start(f32[5,8,256]{2,1,0:T(8,128)} %get-tuple-element.37), channel_id=1, source_target_pairs={{31,0},{24,1},{25,2},{26,3},{27,4},{28,5},{29,6},{30,7},{7,8},{0,9... | collective-permute-start | bytes 122888 | tf_op jit(solution)/shard_map/ppermute | solution.py:39
  13.2 0.0 copy-done
  13.2 0.0 copy-done.1
  13.2 8.4 %spread.4 = (f32[32,32,256]{2,1,0:T(8,128)S(1)}, f32[8,32,256]{2,1,0:T(8,128)}) custom-call(s32[512]{0:T(512)} %refs_0_.11, f32[3,32768]{1,0:T(4,128)S(1)} %copy-done, s32[2,32768]{1,0:T(2,128)S(1)} %copy-done.1, s32[256,128]{1,0:T(8,128)} %bitcast.11, f32[256,128]{1,0:T(8,128)} %bitcast.17, f32[32,8,256]{2,1,0:T(8,128)S(1)} %get-tuple-element.31.refs_5_, ...), custom_call_target="tpu_custom_call" | custom-call | tf_op jit(solution)/shard_map/spread/pallas_call | solution.py:259
  21.6 0.0 collective-permute-done.rim_y_ref
  21.6 0.0 copy-done.2
  21.6 0.0 copy-done.3
  21.6 1.6 forward_z.2
  23.2 0.0 collective-permute-done.2.refs_1_
  23.2 0.0 collective-permute-done.1.refs_0_
  23.2 3.8 %all-to-all-start.1 = ((f32[32,8,1024]{2,1,0:T(8,128)}), f32[32,8,1024]{2,1,0:T(8,128)S(1)}, u32[]{:S(2)}, u32[]{:S(2)}) async-start(f32[32,8,1024]{2,1,0:T(8,128)} %bitcast.4), calls=%async_computation.1 | async-start | bytes 2097152 | tf_op jit(solution)/shard_map/all_to_all | solution.py:669
  27.0 6.3 %spread.5.core_ref = f32[32,32,256]{2,1,0:T(8,128)S(1)} custom-call(s32[512]{0:T(512)} %refs_0_.11, f32[3,32768]{1,0:T(4,128)S(1)} %copy-done, s32[2,32768]{1,0:T(2,128)S(1)} %copy-done.1, s32[256,128]{1,0:T(8,128)} %bitcast.12, f32[256,128]{1,0:T(8,128)} %bitcast.18, f32[8,32,256]{2,1,0:T(8,128)} %get-tuple-element.38.refs_5_, ...), custom_call_target="tpu_custom_call" | custom-call | tf_op jit(solution)/shard_map/spread/pallas_call | solution.py:259
  33.3 1.6 forward_z.3
  34.9 17.4 %all-to-all-done.1.in_ref = f32[32,8,1024]{2,1,0:T(8,128)S(1)} async-done(((f32[32,8,1024]{2,1,0:T(8,128)}), f32[32,8,1024]{2,1,0:T(8,128)S(1)}, u32[]{:S(2)}, u32[]{:S(2)}) %all-to-all-start.1) | async-done | bytes 1048608 | tf_op jit(solution)/shard_map/all_to_all | solution.py:669
  52.3 4.5 %all-to-all-start = ((f32[32,8,1024]{2,1,0:T(8,128)}), f32[32,8,1024]{2,1,0:T(8,128)S(1)}, u32[]{:S(2)}, u32[]{:S(2)}) async-start(f32[32,8,1024]{2,1,0:T(8,128)} %bitcast.3), calls=%async_computation | async-start | bytes 2097152 | tf_op jit(solution)/shard_map/all_to_all | solution.py:669
  56.8 4.5 %planes_first.1 = (f32[2,1024,128]{2,1,0:T(8,128)}, f32[2,1024,128]{2,1,0:T(8,128)}) custom-call(f32[32,8,1024]{2,1,0:T(8,128)S(1)} %all-to-all-done.1.in_ref, bf16[256,512]{1,0:T(8,128)(2,1)} %constant.35.y_high_ref, bf16[256,512]{1,0:T(8,128)(2,1)} %constant.38.y_low_ref), custom_call_target="tpu_custom_call" | custom-call | tf_op jit(solution)/shard_map/planes_first/pallas_call | solution.py:699
  61.3 20.8 %all-to-all-done.in_ref = f32[32,8,1024]{2,1,0:T(8,128)S(1)} async-done(((f32[32,8,1024]{2,1,0:T(8,128)}), f32[32,8,1024]{2,1,0:T(8,128)S(1)}, u32[]{:S(2)}, u32[]{:S(2)}) %all-to-all-start) | async-done | bytes 1048608 | tf_op jit(solution)/shard_map/all_to_all | solution.py:669
  82.1 12.0 %planes.1 = (f32[32,8,1024]{2,1,0:T(8,128)}, f32[2,1024,128]{2,1,0:T(8,128)}, f32[8,128]{1,0:T(8,128)}) custom-call(s32[1]{0:T(128)} %bitcast.2.where_ref, f32[2,256]{1,0:T(2,128)} %constant.30.clone.line_ref, f32[32,8,1024]{2,1,0:T(8,128)S(1)} %all-to-all-done.in_ref, f32[2,1024,128]{2,1,0:T(8,128)} %get-tuple-element.43.far_ref, ...), custom_call_target="tpu_custom_call" | custom-call | tf_op jit(solution)/shard_map/planes/pallas_call | solution.py:707
  94.1 4.5 %all-to-all-start.2 = ((f32[32,8,1024]{2,1,0:T(8,128)}), f32[32,8,1024]{2,1,0:T(8,128)S(1)}, u32[]{:S(2)}, u32[]{:S(2)}) async-start(f32[32,8,1024]{2,1,0:T(8,128)} %get-tuple-element.45), calls=%async_computation.2 | async-start | bytes 2097152 | tf_op jit(solution)/shard_map/all_to_all | solution.py:669
  98.7 4.5 %planes_last.1 = f32[32,8,1152]{2,1,0:T(8,128)} custom-call(f32[2,1024,128]{2,1,0:T(8,128)} %get-tuple-element.47.main_ref, f32[8,128]{1,0:T(8,128)} %get-tuple-element.48.energy_ref, bf16[256,512]{1,0:T(8,128)(2,1)} %constant.35.y_high_ref, bf16[256,512]{1,0:T(8,128)(2,1)} %constant.38.y_low_ref), custom_call_target="tpu_custom_call" | custom-call | tf_op jit(solution)/shard_map/planes_last/pallas_call | solution.py:719
  103.2 20.8 %all-to-all-done.2 = f32[32,8,1024]{2,1,0:T(8,128)S(1)} async-done(((f32[32,8,1024]{2,1,0:T(8,128)}), f32[32,8,1024]{2,1,0:T(8,128)S(1)}, u32[]{:S(2)}, u32[]{:S(2)}) %all-to-all-start.2) | async-done | bytes 1048608 | tf_op jit(solution)/shard_map/all_to_all | solution.py:669
  124.0 4.5 %all-to-all-start.3 = ((f32[32,8,1152]{2,1,0:T(8,128)}), f32[32,8,1152]{2,1,0:T(8,128)S(1)}, u32[]{:S(2)}, u32[]{:S(2)}) async-start(f32[32,8,1152]{2,1,0:T(8,128)} %planes_last.1), calls=%async_computation.3 | async-start | bytes 2359296 | tf_op jit(solution)/shard_map/all_to_all | solution.py:669
  128.5 2.5 %backward_z.2 = (f32[32,32,256]{2,1,0:T(8,128)S(1)}, f32[32,8,256]{2,1,0:T(8,128)}, f32[5,32,256]{2,1,0:T(8,128)}, f32[5,8,256]{2,1,0:T(8,128)}, f32[8,32,256]{2,1,0:T(8,128)}) custom-call(f32[256,1024]{1,0:T(8,128)S(1)} %bitcast.9, bf16[256,256]{1,0:T(8,128)(2,1)} %constant.45.high_ref, bf16[256,256]{1,0:T(8,128)(2,1)} %constant.48.low_ref), custom_call_target="tpu_custom_call" | custom-call | tf_op jit(solution)/shard_map/backward_z/pallas_call | solution.py:465
  131.0 2.1 %collective-permute-start.3 = (f32[32,8,256]{2,1,0:T(8,128)}, f32[32,8,256]{2,1,0:T(8,128)S(1)}, u32[]{:S(2)}, u32[]{:S(2)}) collective-permute-start(f32[32,8,256]{2,1,0:T(8,128)} %get-tuple-element.50), channel_id=1, source_target_pairs={{1,0},{2,1},{3,2},{4,3},{5,4},{6,5},{7,6},{0,7},{9,8},{10,9},{11,1... | collective-permute-start | bytes 786440 | tf_op jit(solution)/shard_map/ppermute | solution.py:29
  133.1 0.6 collective-permute-start.4
  133.6 2.9 %collective-permute-start.5 = (f32[5,8,256]{2,1,0:T(8,128)}, f32[5,8,256]{2,1,0:T(8,128)S(1)}, u32[]{:S(2)}, u32[]{:S(2)}) collective-permute-start(f32[5,8,256]{2,1,0:T(8,128)} %get-tuple-element.52), channel_id=1, source_target_pairs={{9,0},{10,1},{11,2},{12,3},{13,4},{14,5},{15,6},{8,7},{17,8},{18,9... | collective-permute-start | bytes 122888 | tf_op jit(solution)/shard_map/ppermute | solution.py:39
  136.5 2.6 %collective-permute-done.3.refs_6_.refs_8_ = f32[32,8,256]{2,1,0:T(8,128)S(1)} collective-permute-done((f32[32,8,256]{2,1,0:T(8,128)}, f32[32,8,256]{2,1,0:T(8,128)S(1)}, u32[]{:S(2)}, u32[]{:S(2)}) %collective-permute-start.3) | collective-permute-done | bytes 262176 | tf_op jit(solution)/shard_map/ppermute | solution.py:29
  139.2 9.8 %interpolate.3.refs_11_ = f32[3,12288]{1,0:T(4,128)} custom-call(s32[512]{0:T(512)} %refs_0_.11, f32[3,32768]{1,0:T(4,128)S(1)} %copy-done, s32[2,32768]{1,0:T(2,128)S(1)} %copy-done.1, s32[256,128]{1,0:T(8,128)} %bitcast.13, f32[256,128]{1,0:T(8,128)} %bitcast.19, f32[32,32,256]{2,1,0:T(8,128)S(1)} %get-tuple-element.49.refs_5_, ...), custom_call_target="tpu_custom_call" | custom-call | tf_op jit(solution)/shard_map/interpolate/pallas_call | solution.py:347
  149.0 11.1 %collective-permute-done.5.refs_10_ = f32[5,8,256]{2,1,0:T(8,128)S(1)} collective-permute-done((f32[5,8,256]{2,1,0:T(8,128)}, f32[5,8,256]{2,1,0:T(8,128)S(1)}, u32[]{:S(2)}, u32[]{:S(2)}) %collective-permute-start.5) | collective-permute-done | bytes 40992 | tf_op jit(solution)/shard_map/ppermute | solution.py:39
  160.1 0.1 collective-permute-done.4.refs_7_
  160.3 0.0 all-to-all-done.3
  160.3 2.4 %backward_z.3 = (f32[32,32,256]{2,1,0:T(8,128)S(1)}, f32[32,8,256]{2,1,0:T(8,128)}, f32[1]{0:T(128)}) custom-call(f32[256,1152]{1,0:T(8,128)S(1)} %bitcast.8, bf16[256,256]{1,0:T(8,128)(2,1)} %constant.45.high_ref, bf16[256,256]{1,0:T(8,128)(2,1)} %constant.48.low_ref), custom_call_target="tpu_custom_call" | custom-call | tf_op jit(solution)/shard_map/backward_z/pallas_call | solution.py:465
  162.7 2.3 %collective-permute-start.6 = (f32[32,8,256]{2,1,0:T(8,128)}, f32[32,8,256]{2,1,0:T(8,128)S(1)}, u32[]{:S(2)}, u32[]{:S(2)}) collective-permute-start(f32[32,8,256]{2,1,0:T(8,128)} %get-tuple-element.56), channel_id=1, source_target_pairs={{1,0},{2,1},{3,2},{4,3},{5,4},{6,5},{7,6},{0,7},{9,8},{10,9},{11,1... | collective-permute-start | bytes 786440 | tf_op jit(solution)/shard_map/ppermute | solution.py:29
  164.9 11.3 %interpolate.4.refs_12_ = f32[3,20480]{1,0:T(4,128)S(1)} custom-call(s32[512]{0:T(512)} %refs_0_.11, f32[3,32768]{1,0:T(4,128)S(1)} %copy-done, s32[2,32768]{1,0:T(2,128)S(1)} %copy-done.1, s32[256,128]{1,0:T(8,128)} %bitcast.14, f32[256,128]{1,0:T(8,128)} %bitcast.20, f32[8,32,256]{2,1,0:T(8,128)} %get-tuple-element.46.refs_5_, ...), custom_call_target="tpu_custom_call" | custom-call | tf_op jit(solution)/shard_map/interpolate/pallas_call | solution.py:347
  176.2 0.0 collective-permute-done.6.refs_9_
  176.2 5.3 %interpolate.5 = f32[3,32768]{1,0:T(4,128)} custom-call(s32[512]{0:T(512)} %refs_0_.11, f32[3,32768]{1,0:T(4,128)S(1)} %copy-done, s32[2,32768]{1,0:T(2,128)S(1)} %copy-done.1, s32[256,128]{1,0:T(8,128)} %bitcast.15, f32[256,128]{1,0:T(8,128)} %bitcast.21, f32[8,32,256]{2,1,0:T(8,128)} %get-tuple-element.46.refs_5_, ...), custom_call_target="tpu_custom_call" | custom-call | tf_op jit(solution)/shard_map/interpolate/pallas_call | solution.py:347
Async XLA Ops:
  0.6 12.6 %copy-start = (f32[3,32768]{1,0:T(4,128)S(1)}, f32[3,32768]{1,0:T(4,128)}, u32[]{:S(2)}) copy-start(f32[3,32768]{1,0:T(4,128)} %refs_1_.11) | copy-start | bytes 1179652
  0.6 12.6 %copy-start.1 = (s32[2,32768]{1,0:T(2,128)S(1)}, s32[2,32768]{1,0:T(2,128)}, u32[]{:S(2)}) copy-start(s32[2,32768]{1,0:T(2,128)} %refs_2_.11) | copy-start | bytes 786436
  0.6 20.9 %copy-start.2 = (bf16[256,256]{1,0:T(8,128)(2,1)S(1)}, bf16[256,256]{1,0:T(8,128)(2,1)}, u32[]{:S(2)}) copy-start(bf16[256,256]{1,0:T(8,128)(2,1)} %constant.34.refs_1_.refs_3_) | copy-start | bytes 393220
  0.7 20.9 %copy-start.3 = (bf16[256,256]{1,0:T(8,128)(2,1)S(1)}, bf16[256,256]{1,0:T(8,128)(2,1)}, u32[]{:S(2)}) copy-start(bf16[256,256]{1,0:T(8,128)(2,1)} %constant.31.refs_0_.refs_2_) | copy-start | bytes 393220
  9.1 12.5 %collective-permute-start = (f32[64,8,256]{2,1,0:T(8,128)}, f32[64,8,256]{2,1,0:T(8,128)S(1)}, u32[]{:S(2)}, u32[]{:S(2)}) collective-permute-start(f32[64,8,256]{2,1,0:T(8,128)} %get-tuple-element.35), channel_id=1, source_target_pairs={{7,0},{0,1},{1,2},{2,3},{3,4},{4,5},{5,6},{6,7},{15,8},{8,9},{9,10... | collective-permute-start | bytes 1572872 | tf_op jit(solution)/shard_map/ppermute | solution.py:29
  9.1 14.1 %collective-permute-start.1 = (f32[5,32,256]{2,1,0:T(8,128)}, f32[5,32,256]{2,1,0:T(8,128)S(1)}, u32[]{:S(2)}, u32[]{:S(2)}) collective-permute-start(f32[5,32,256]{2,1,0:T(8,128)} %get-tuple-element.36), channel_id=1, source_target_pairs={{24,0},{0,8},{8,16},{16,24},{25,1},{1,9},{9,17},{17,25},{26,2},{2,... | collective-permute-start | bytes 491528 | tf_op jit(solution)/shard_map/ppermute | solution.py:29
  10.7 12.5 %collective-permute-start.2 = (f32[5,8,256]{2,1,0:T(8,128)}, f32[5,8,256]{2,1,0:T(8,128)S(1)}, u32[]{:S(2)}, u32[]{:S(2)}) collective-permute-start(f32[5,8,256]{2,1,0:T(8,128)} %get-tuple-element.37), channel_id=1, source_target_pairs={{31,0},{24,1},{25,2},{26,3},{27,4},{28,5},{29,6},{30,7},{7,8},{0,9... | collective-permute-start | bytes 122888 | tf_op jit(solution)/shard_map/ppermute | solution.py:39
  23.2 29.1 %all-to-all-start.1 = ((f32[32,8,1024]{2,1,0:T(8,128)}), f32[32,8,1024]{2,1,0:T(8,128)S(1)}, u32[]{:S(2)}, u32[]{:S(2)}) async-start(f32[32,8,1024]{2,1,0:T(8,128)} %bitcast.4), calls=%async_computation.1 | async-start | bytes 2097152 | tf_op jit(solution)/shard_map/all_to_all | solution.py:669
  52.3 29.8 %all-to-all-start = ((f32[32,8,1024]{2,1,0:T(8,128)}), f32[32,8,1024]{2,1,0:T(8,128)S(1)}, u32[]{:S(2)}, u32[]{:S(2)}) async-start(f32[32,8,1024]{2,1,0:T(8,128)} %bitcast.3), calls=%async_computation | async-start | bytes 2097152 | tf_op jit(solution)/shard_map/all_to_all | solution.py:669
  94.1 29.8 %all-to-all-start.2 = ((f32[32,8,1024]{2,1,0:T(8,128)}), f32[32,8,1024]{2,1,0:T(8,128)S(1)}, u32[]{:S(2)}, u32[]{:S(2)}) async-start(f32[32,8,1024]{2,1,0:T(8,128)} %get-tuple-element.45), calls=%async_computation.2 | async-start | bytes 2097152 | tf_op jit(solution)/shard_map/all_to_all | solution.py:669
  124.0 36.3 %all-to-all-start.3 = ((f32[32,8,1152]{2,1,0:T(8,128)}), f32[32,8,1152]{2,1,0:T(8,128)S(1)}, u32[]{:S(2)}, u32[]{:S(2)}) async-start(f32[32,8,1152]{2,1,0:T(8,128)} %planes_last.1), calls=%async_computation.3 | async-start | bytes 2359296 | tf_op jit(solution)/shard_map/all_to_all | solution.py:669
  131.0 8.2 %collective-permute-start.3 = (f32[32,8,256]{2,1,0:T(8,128)}, f32[32,8,256]{2,1,0:T(8,128)S(1)}, u32[]{:S(2)}, u32[]{:S(2)}) collective-permute-start(f32[32,8,256]{2,1,0:T(8,128)} %get-tuple-element.50), channel_id=1, source_target_pairs={{1,0},{2,1},{3,2},{4,3},{5,4},{6,5},{7,6},{0,7},{9,8},{10,9},{11,1... | collective-permute-start | bytes 786440 | tf_op jit(solution)/shard_map/ppermute | solution.py:29
  133.1 27.2 %collective-permute-start.4 = (f32[5,32,256]{2,1,0:T(8,128)}, f32[5,32,256]{2,1,0:T(8,128)S(1)}, u32[]{:S(2)}, u32[]{:S(2)}) collective-permute-start(f32[5,32,256]{2,1,0:T(8,128)} %get-tuple-element.51), channel_id=1, source_target_pairs={{8,0},{16,8},{24,16},{0,24},{9,1},{17,9},{25,17},{1,25},{10,2},{18... | collective-permute-start | bytes 491528 | tf_op jit(solution)/shard_map/ppermute | solution.py:29
  133.6 26.5 %collective-permute-start.5 = (f32[5,8,256]{2,1,0:T(8,128)}, f32[5,8,256]{2,1,0:T(8,128)S(1)}, u32[]{:S(2)}, u32[]{:S(2)}) collective-permute-start(f32[5,8,256]{2,1,0:T(8,128)} %get-tuple-element.52), channel_id=1, source_target_pairs={{9,0},{10,1},{11,2},{12,3},{13,4},{14,5},{15,6},{8,7},{17,8},{18,9... | collective-permute-start | bytes 122888 | tf_op jit(solution)/shard_map/ppermute | solution.py:39
  162.7 13.5 %collective-permute-start.6 = (f32[32,8,256]{2,1,0:T(8,128)}, f32[32,8,256]{2,1,0:T(8,128)S(1)}, u32[]{:S(2)}, u32[]{:S(2)}) collective-permute-start(f32[32,8,256]{2,1,0:T(8,128)} %get-tuple-element.56), channel_id=1, source_target_pairs={{1,0},{2,1},{3,2},{4,3},{5,4},{6,5},{7,6},{0,7},{9,8},{10,9},{11,1... | collective-permute-start | bytes 786440 | tf_op jit(solution)/shard_map/ppermute | solution.py:29

commit v3 on v2

--- a/solution.py
+++ b/solution.py
@@ -116,18 +116,8 @@
     return sum((last - first) * (high - low) for first, last, low, high in ranges) // 4
 
 
-def step_atoms(places, refs, slots, groups):
-    counts_ref, frac_ref, offs_ref, z_ref, q_ref = refs
+def live_part(charge, counts_ref, lines, slots):
     per_row = LANES // slots
-    lines = [(a * groups + g) * 2 + half for a, g in places for half in range(2)]
-
-    def wide(ref, d):
-        rows = [ref[d : d + 1, pl.ds(pl.multiple_of(line * LANES, LANES), LANES)] for line in lines]
-        return jnp.concatenate(rows, axis=0)
-
-    def tall(ref):
-        return jnp.concatenate([ref[pl.ds(line, 1), :] for line in lines], axis=0)
-
     row_at = lax.broadcasted_iota(jnp.int32, (8, LANES), 0)
     lane_at = lax.broadcasted_iota(jnp.int32, (8, LANES), 1)
     tile_at = row_at * per_row + lane_at // slots
@@ -135,7 +125,26 @@
     for r, line in enumerate(lines):
         for k in range(per_row):
             count = jnp.where(tile_at == r * per_row + k, counts_ref[line * per_row + k], count)
-    charge = jnp.where(lane_at % slots < count, tall(q_ref), 0.0)
+    return jnp.where(lane_at % slots < count, charge, 0.0)
+
+
+def step_atoms(places, refs, slots, groups):
+    frac_ref, offs_ref, z_ref, q_ref = refs[-4:]
+    per_row = LANES // slots
+    lines = [(a * groups + g) * 2 + half for a, g in places for half in range(2)]
+
+    def wide(ref, d):
+        rows = [ref[d : d + 1, pl.ds(pl.multiple_of(line * LANES, LANES), LANES)] for line in lines]
+        return jnp.concatenate(rows, axis=0)
+
+    def tall(ref):
+        return jnp.concatenate([ref[pl.ds(line, 1), :] for line in lines], axis=0)
+
+    row_at = lax.broadcasted_iota(jnp.int32, (8, LANES), 0)
+    lane_at = lax.broadcasted_iota(jnp.int32, (8, LANES), 1)
+    charge = tall(q_ref)
+    if len(refs) == 5:
+        charge = live_part(charge, refs[0], lines, slots)
     tile_in_group = (row_at % 2) * per_row + lane_at // slots
     fracs = [wide(frac_ref, d) for d in range(3)]
     return fracs, wide(offs_ref, 0), wide(offs_ref, 1) + 2 * tile_in_group, tall(z_ref), charge, lines
@@ -175,15 +184,15 @@
     )
 
 
-def spread_body(*refs, slots, groups, ranges, base, pieces, carried):
-    atom_refs = refs[:5]
+def spread_body(*refs, slots, groups, ranges, base, pieces, carried, given, emit):
+    atom_refs = refs[:given]
     acc_ref, tab_ref = refs[-2:]
     acc_ref[...] = jnp.zeros_like(acc_ref)
     clear_rows(tab_ref)
-    for piece, ref in zip(carried, refs[5:]):
+    for piece, ref in zip(carried, refs[given:]):
         low = (piece[0] - base, piece[2])
         acc_ref[low[0] : low[0] + ref.shape[0], low[1] : low[1] + ref.shape[1]] += ref[...]
-    refs = refs[5 + len(carried) :]
+    refs = refs[given + len(carried) :]
     at = lax.broadcasted_iota(jnp.int32, (ROWS, LANES), 0)
 
     def body(step, carry):
@@ -222,6 +231,17 @@
         return carry
 
     lax.fori_loop(0, step_count(ranges), body, 0)
+    if emit:
+        z_out_ref, live_ref = refs[len(pieces) : len(pieces) + 2]
+        z_out_ref[...] = atom_refs[3][...]
+
+        def live_body(step, carry):
+            rows = pl.ds(pl.multiple_of(8 * step, 8), 8)
+            lines = [8 * step + r for r in range(8)]
+            live_ref[rows, :] = live_part(atom_refs[4][rows, :], atom_refs[0], lines, slots)
+            return carry
+
+        lax.fori_loop(0, live_ref.shape[0] // 8, live_body, 0)
     for piece, ref in zip(pieces, refs):
         ref[...] = acc_ref[piece[0] - base : piece[1] - base, piece[2] : piece[3], :]
 
@@ -249,17 +269,21 @@
 smem = pl.BlockSpec(memory_space=pltpu.SMEM)
 
 
-def spread_charges(atoms, slots, groups, block_y, ranges, pieces, holds, carried=(), fields=()):
+def spread_charges(atoms, slots, groups, block_y, ranges, pieces, holds, carried=(), fields=(), emit=False):
     base = min([2 * r[0] for r in ranges] + [p[0] for p in pieces + list(carried)])
     top = max([2 * r[1] + REACH for r in ranges] + [p[1] for p in pieces + list(carried)])
     body = functools.partial(
-        spread_body, slots=slots, groups=groups, ranges=ranges, base=base, pieces=pieces, carried=carried
+        spread_body, slots=slots, groups=groups, ranges=ranges, base=base, pieces=pieces, carried=carried,
+        given=len(atoms), emit=emit,
     )
     shapes = [(p[1] - p[0], p[3] - p[2], KZ) for p in pieces]
+    shapes = [hold(s) for hold, s in zip(holds, shapes)]
+    if emit:
+        shapes += [pltpu.VMEM(atoms[3].shape, jnp.int32), kept(atoms[4].shape)]
     return pl.pallas_call(
         body,
-        out_shape=[hold(s) for hold, s in zip(holds, shapes)],
-        in_specs=[smem] + [vmem] * (4 + len(fields)),
+        out_shape=shapes,
+        in_specs=[smem] * (len(atoms) - 4) + [vmem] * (4 + len(fields)),
         compiler_params=room,
         out_specs=[vmem] * len(shapes),
         scratch_shapes=[pltpu.VMEM((top - base, block_y + 8, KZ), f32), pltpu.VMEM((128, LANES), f32)],
@@ -469,7 +493,7 @@
         compiler_params=room,
         out_specs=[vmem] * (1 + len(sent)) + [smem] * len(total),
         name="backward_z",
-    )(*resident([spectral]), *apart([high, low]))
+    )(*resident([spectral]), high, low)
 
 
 def swap_blocks(parts, width):
@@ -561,8 +585,12 @@
     lax.fori_loop(0, groups * spans, body, 0)
 
 
-def planes_first_body(in_ref, y_high_ref, y_low_ref, main_ref, twin_ref, *, pens, width):
+def planes_first_body(in_ref, y_high_ref, y_low_ref, main_ref, pair_ref, twin_ref, *, pens, width):
     forward_y(in_ref, y_high_ref, y_low_ref, main_ref, twin_ref, pens, width)
+    count = twin_ref.shape[1] // 8
+    for k in range(2):
+        for part in range(2):
+            pair_ref[k, part * count : (part + 1) * count, :] = twin_ref[k, pl.ds(4 * part, count, stride=8), :]
 
 
 def planes_last_body(main_ref, energy_ref, y_high_ref, y_low_ref, out_ref, *, pens, width, lines):
@@ -594,7 +622,12 @@
         def whole(ref):
             return jnp.concatenate([ref[k, pl.ds(comp, ref.shape[1] // 8, stride=8), :] for k in range(2)], axis=1)
 
-        return jnp.concatenate([whole(near_ref), whole(far_ref)], axis=0)
+        if far_ref is None:
+            rows = slice(comp // 4 * (KX - near), (comp // 4 + 1) * (KX - near))
+            far_rows = jnp.concatenate([far_twin_ref[k, rows, :] for k in range(2)], axis=1)
+        else:
+            far_rows = whole(far_ref)
+        return jnp.concatenate([whole(near_ref), far_rows], axis=0)
 
     def influence(entry):
         square = column_ref[0] + (row_ref[0] + line_ref[0, entry])
@@ -610,9 +643,7 @@
             other = influence(KZ // 2)
             share = jnp.where(mine, 0.5 * (kernel + other), kernel)
             cross = jnp.where(mine, 0.5 * (kernel - other), 0.0)
-            twin_real, twin_imag = times_x(
-                plane_of(twin_ref, far_twin_ref, 0), plane_of(twin_ref, far_twin_ref, 4)
-            )
+            twin_real, twin_imag = times_x(plane_of(twin_ref, None, 0), plane_of(twin_ref, None, 4))
             out_real = share * real + cross * twin_real
             out_imag = share * imag + cross * twin_imag
             energy = energy + jnp.where(mine, 0.5, 1.0) * (real * out_real + imag * out_imag)
@@ -675,8 +706,8 @@
     ]
     carried = [(0, half, edge_y, block_y), (half, block_x, edge_y, block_y), (2 * late, block_x, 0, edge_y)]
     ranges = [(0, tiles_x, inner, groups), (late, tiles_x, 0, inner)]
-    rim_y, rim_x, corner, near_edge, far_edge, end = spread_charges(
-        atoms, *sizes, ranges, rim_pieces + carried, [stored] * 4 + [kept] * 2
+    rim_y, rim_x, corner, near_edge, far_edge, end, z_kept, live = spread_charges(
+        atoms, *sizes, ranges, rim_pieces + carried, [stored] * 4 + [kept] * 2, emit=True
     )
     rim_y = shifted(rim_y, "pen", 1)
     rim_x = shifted(rim_x, "grp", 1)
@@ -684,7 +715,7 @@
     pieces = [(half, block_x, 0, block_y), (2 * cut, half, 0, block_y)]
     atoms = [atoms[0], *resident(atoms[1:3]), *atoms[3:]]
     core, over = spread_charges(
-        atoms, *sizes, [(cut, late, 0, inner)], pieces, [kept, stored], carried[1:], resident([far_edge, end])
+        [*atoms[1:3], *resident([z_kept, live])], *sizes, [(cut, late, 0, inner)], pieces, [kept, stored], carried[1:], resident([far_edge, end])
     )
     far = forward_z(core, (rim_y,), *forward, half)
     over, far, rim_x, corner = lax.optimization_barrier((over, far, rim_x, corner))
@@ -698,7 +729,8 @@
     part = stored((2, KX // 2 * 8, LANES))
     far, far_twin = pl.pallas_call(
         functools.partial(planes_first_body, pens=pens, width=block_y),
-        out_shape=[part, part],
+        out_shape=[part, stored((2, KX, LANES))],
+        scratch_shapes=[pltpu.VMEM((2, KX // 2 * 8, LANES), f32)],
         in_specs=[vmem] * 3,
         compiler_params=room,
         out_specs=[vmem] * 2,

time: 182 us -> 181 us (level)
  Pallas kernels: 78.6 us -> 75.8 us
    pallas_call x2, Pallas kernels: 4.85 us -> 2.91 us  [backward_z(): pl.pallas_call(functools.partial(backward_z_body, chunk=chunk, scale=scal...]
  transfers between devices with their start and end apart: 11 -> 11, of which waited for: 6 -> 6; matrix products, arithmetic and copies ran while one was open for 0% -> 0% of each run, Pallas kernels for 28% -> 27%
where the time goes in v3:
time: 181 us; the launch traced here: 180 us
  Pallas kernels  75.8 us (42%)
  waiting for transfers between devices  74.1 us (41%)
  starting transfers between devices  29.3 us (16%)
    all_to_all x4, waiting for transfers between devices, exchange(): lax.all_to_all(spectral.reshape(devices, 8, -1), axes, 0, 0, tiled=True)  59.2 us
    pallas_call x3, Pallas kernels, interpolate(): pl.pallas_call(body, out_shape=hold((3, (rows[1] - rows[0]) * line * LANE...  26.3 us
    pallas_call x3, Pallas kernels, spread_charges(): pl.pallas_call(body, out_shape=shapes, in_specs=[smem] * (len(atoms) - 4)...  22.9 us
    all_to_all x4, starting transfers between devices, exchange(): lax.all_to_all(spectral.reshape(devices, 8, -1), axes, 0, 0, tiled=True)  17.4 us
    pallas_call x1, Pallas kernels, by_halves(): pl.pallas_call(functools.partial(planes_body, pens=pens, width=block_y),...  11.8 us
    ppermute x2, waiting for transfers between devices, shifted_both(): return lax.ppermute(block, ('grp', 'pen'), route)  11.2 us
    ppermute x5, starting transfers between devices, shifted(): return lax.ppermute(block, axis, route)  6.51 us
    ppermute x2, starting transfers between devices, shifted_both(): return lax.ppermute(block, ('grp', 'pen'), route)  5.41 us
  transfers between devices with their start and end apart: 11, of which 6 were waited for; matrix products, arithmetic and copies ran while one was open for 0% of the time, Pallas kernels for 27%

profile of v3, /device:TPU:8, one launch (start us, length us, event | category | flops | bytes accessed | tf_op | source)
XLA Modules:
  0.0 180.0 jit_solution(10143155884789688566)
XLA Ops:
  0.6 0.0 copy-start
  0.6 0.0 copy-start.1
  0.6 0.0 copy-start.2
  0.7 0.0 copy-start.3
  0.7 9.0 %spread.3 = (f32[64,8,256]{2,1,0:T(8,128)}, f32[5,32,256]{2,1,0:T(8,128)}, f32[5,8,256]{2,1,0:T(8,128)}, f32[32,8,256]{2,1,0:T(8,128)}, f32[32,8,256]{2,1,0:T(8,...) custom-call(s32[512]{0:T(512)} %refs_0_.11, f32[3,32768]{1,0:T(4,128)} %refs_1_.11, ...), custom_call_target="tpu_custom_call" | custom-call | tf_op jit(solution)/shard_map/spread/pallas_call | solution.py:283
  9.6 0.0 collective-permute-start
  9.7 1.6 collective-permute-start.1
  11.2 2.5 %collective-permute-start.2 = (f32[5,8,256]{2,1,0:T(8,128)}, f32[5,8,256]{2,1,0:T(8,128)S(1)}, u32[]{:S(2)}, u32[]{:S(2)}) collective-permute-start(f32[5,8,256]{2,1,0:T(8,128)} %get-tuple-element.41), channel_id=1, source_target_pairs={{31,0},{24,1},{25,2},{26,3},{27,4},{28,5},{29,6},{30,7},{7,8},{0,9... | collective-permute-start | bytes 122888 | tf_op jit(solution)/shard_map/ppermute | solution.py:39
  13.7 0.0 copy-done
  13.7 0.0 copy-done.1
  13.7 7.6 %spread.4 = (f32[32,32,256]{2,1,0:T(8,128)S(1)}, f32[8,32,256]{2,1,0:T(8,128)}) custom-call(f32[3,32768]{1,0:T(4,128)S(1)} %copy-done, s32[2,32768]{1,0:T(2,128)S(1)} %copy-done.1, s32[256,128]{1,0:T(8,128)S(1)} %get-tuple-element.33.refs_2_, f32[256,128]{1,0:T(8,128)S(1)} %get-tuple-element.34.refs_3_, f32[32,8,256]{2,1,0:T(8,128)S(1)} %get-tuple-element.35.refs_4_, ...), custom_call_target="tpu_custom_call" | custom-call | tf_op jit(solution)/shard_map/spread/pallas_call | solution.py:283
  21.4 0.0 collective-permute-done.rim_y_ref
  21.4 0.0 copy-done.2
  21.4 0.0 copy-done.3
  21.4 1.6 forward_z.2
  23.0 0.0 collective-permute-done.2.refs_1_
  23.0 0.0 collective-permute-done.1.refs_0_
  23.0 3.8 %all-to-all-start.1 = ((f32[32,8,1024]{2,1,0:T(8,128)}), f32[32,8,1024]{2,1,0:T(8,128)S(1)}, u32[]{:S(2)}, u32[]{:S(2)}) async-start(f32[32,8,1024]{2,1,0:T(8,128)} %bitcast.4), calls=%async_computation.1 | async-start | bytes 2097152 | tf_op jit(solution)/shard_map/all_to_all | solution.py:700
  26.8 6.3 %spread.5.core_ref = f32[32,32,256]{2,1,0:T(8,128)S(1)} custom-call(s32[512]{0:T(512)} %refs_0_.11, f32[3,32768]{1,0:T(4,128)S(1)} %copy-done, s32[2,32768]{1,0:T(2,128)S(1)} %copy-done.1, s32[256,128]{1,0:T(8,128)} %bitcast.11, f32[256,128]{1,0:T(8,128)} %bitcast.16, f32[8,32,256]{2,1,0:T(8,128)} %get-tuple-element.42.refs_5_, ...), custom_call_target="tpu_custom_call" | custom-call | tf_op jit(solution)/shard_map/spread/pallas_call | solution.py:283
  33.1 1.6 forward_z.3
  34.7 17.4 %all-to-all-done.1.in_ref = f32[32,8,1024]{2,1,0:T(8,128)S(1)} async-done(((f32[32,8,1024]{2,1,0:T(8,128)}), f32[32,8,1024]{2,1,0:T(8,128)S(1)}, u32[]{:S(2)}, u32[]{:S(2)}) %all-to-all-start.1) | async-done | bytes 1048608 | tf_op jit(solution)/shard_map/all_to_all | solution.py:700
  52.1 4.5 %all-to-all-start = ((f32[32,8,1024]{2,1,0:T(8,128)}), f32[32,8,1024]{2,1,0:T(8,128)S(1)}, u32[]{:S(2)}, u32[]{:S(2)}) async-start(f32[32,8,1024]{2,1,0:T(8,128)} %bitcast.3), calls=%async_computation | async-start | bytes 2097152 | tf_op jit(solution)/shard_map/all_to_all | solution.py:700
  56.6 4.2 %planes_first.1 = (f32[2,1024,128]{2,1,0:T(8,128)}, f32[2,256,128]{2,1,0:T(8,128)}) custom-call(f32[32,8,1024]{2,1,0:T(8,128)S(1)} %all-to-all-done.1.in_ref, bf16[256,512]{1,0:T(8,128)(2,1)} %constant.35.y_high_ref, bf16[256,512]{1,0:T(8,128)(2,1)} %constant.38.y_low_ref), custom_call_target="tpu_custom_call" | custom-call | tf_op jit(solution)/shard_map/planes_first/pallas_call | solution.py:730
  60.9 21.0 %all-to-all-done.in_ref = f32[32,8,1024]{2,1,0:T(8,128)S(1)} async-done(((f32[32,8,1024]{2,1,0:T(8,128)}), f32[32,8,1024]{2,1,0:T(8,128)S(1)}, u32[]{:S(2)}, u32[]{:S(2)}) %all-to-all-start) | async-done | bytes 1048608 | tf_op jit(solution)/shard_map/all_to_all | solution.py:700
  81.9 11.8 %planes.1 = (f32[32,8,1024]{2,1,0:T(8,128)}, f32[2,1024,128]{2,1,0:T(8,128)}, f32[8,128]{1,0:T(8,128)}) custom-call(s32[1]{0:T(128)} %bitcast.2.where_ref, f32[2,256]{1,0:T(2,128)} %constant.30.clone.line_ref, f32[32,8,1024]{2,1,0:T(8,128)S(1)} %all-to-all-done.in_ref, f32[2,1024,128]{2,1,0:T(8,128)} %get-tuple-element.47.far_ref, ...), custom_call_target="tpu_custom_call" | custom-call | tf_op jit(solution)/shard_map/planes/pallas_call | solution.py:739
  93.7 4.5 %all-to-all-start.2 = ((f32[32,8,1024]{2,1,0:T(8,128)}), f32[32,8,1024]{2,1,0:T(8,128)S(1)}, u32[]{:S(2)}, u32[]{:S(2)}) async-start(f32[32,8,1024]{2,1,0:T(8,128)} %get-tuple-element.49), calls=%async_computation.2 | async-start | bytes 2097152 | tf_op jit(solution)/shard_map/all_to_all | solution.py:700
  98.2 4.5 %planes_last.1 = f32[32,8,1152]{2,1,0:T(8,128)} custom-call(f32[2,1024,128]{2,1,0:T(8,128)} %get-tuple-element.51.main_ref, f32[8,128]{1,0:T(8,128)} %get-tuple-element.52.energy_ref, bf16[256,512]{1,0:T(8,128)(2,1)} %constant.35.y_high_ref, bf16[256,512]{1,0:T(8,128)(2,1)} %constant.38.y_low_ref), custom_call_target="tpu_custom_call" | custom-call | tf_op jit(solution)/shard_map/planes_last/pallas_call | solution.py:751
  102.8 0.0 copy-start.4
  102.8 0.0 copy-start.5
  102.8 20.7 %all-to-all-done.2 = f32[32,8,1024]{2,1,0:T(8,128)S(1)} async-done(((f32[32,8,1024]{2,1,0:T(8,128)}), f32[32,8,1024]{2,1,0:T(8,128)S(1)}, u32[]{:S(2)}, u32[]{:S(2)}) %all-to-all-start.2) | async-done | bytes 1048608 | tf_op jit(solution)/shard_map/all_to_all | solution.py:700
  123.5 4.5 %all-to-all-start.3 = ((f32[32,8,1152]{2,1,0:T(8,128)}), f32[32,8,1152]{2,1,0:T(8,128)S(1)}, u32[]{:S(2)}, u32[]{:S(2)}) async-start(f32[32,8,1152]{2,1,0:T(8,128)} %planes_last.1), calls=%async_computation.3 | async-start | bytes 2359296 | tf_op jit(solution)/shard_map/all_to_all | solution.py:700
  128.1 0.0 copy-done.4
  128.1 0.0 copy-done.5
  128.1 1.5 backward_z.2
  129.6 2.1 %collective-permute-start.3 = (f32[32,8,256]{2,1,0:T(8,128)}, f32[32,8,256]{2,1,0:T(8,128)S(1)}, u32[]{:S(2)}, u32[]{:S(2)}) collective-permute-start(f32[32,8,256]{2,1,0:T(8,128)} %get-tuple-element.54), channel_id=1, source_target_pairs={{1,0},{2,1},{3,2},{4,3},{5,4},{6,5},{7,6},{0,7},{9,8},{10,9},{11,1... | collective-permute-start | bytes 786440 | tf_op jit(solution)/shard_map/ppermute | solution.py:29
  131.7 0.6 collective-permute-start.4
  132.2 2.9 %collective-permute-start.5 = (f32[5,8,256]{2,1,0:T(8,128)}, f32[5,8,256]{2,1,0:T(8,128)S(1)}, u32[]{:S(2)}, u32[]{:S(2)}) collective-permute-start(f32[5,8,256]{2,1,0:T(8,128)} %get-tuple-element.56), channel_id=1, source_target_pairs={{9,0},{10,1},{11,2},{12,3},{13,4},{14,5},{15,6},{8,7},{17,8},{18,9... | collective-permute-start | bytes 122888 | tf_op jit(solution)/shard_map/ppermute | solution.py:39
  135.1 3.6 %collective-permute-done.3.refs_6_.refs_8_ = f32[32,8,256]{2,1,0:T(8,128)S(1)} collective-permute-done((f32[32,8,256]{2,1,0:T(8,128)}, f32[32,8,256]{2,1,0:T(8,128)S(1)}, u32[]{:S(2)}, u32[]{:S(2)}) %collective-permute-start.3) | collective-permute-done | bytes 262176 | tf_op jit(solution)/shard_map/ppermute | solution.py:29
  138.7 9.8 %interpolate.3.refs_11_ = f32[3,12288]{1,0:T(4,128)} custom-call(s32[512]{0:T(512)} %refs_0_.11, f32[3,32768]{1,0:T(4,128)S(1)} %copy-done, s32[2,32768]{1,0:T(2,128)S(1)} %copy-done.1, s32[256,128]{1,0:T(8,128)} %bitcast.12, f32[256,128]{1,0:T(8,128)} %bitcast.17, f32[32,32,256]{2,1,0:T(8,128)S(1)} %get-tuple-element.53.refs_5_, ...), custom_call_target="tpu_custom_call" | custom-call | tf_op jit(solution)/shard_map/interpolate/pallas_call | solution.py:371
  148.5 11.2 %collective-permute-done.5.refs_10_ = f32[5,8,256]{2,1,0:T(8,128)S(1)} collective-permute-done((f32[5,8,256]{2,1,0:T(8,128)}, f32[5,8,256]{2,1,0:T(8,128)S(1)}, u32[]{:S(2)}, u32[]{:S(2)}) %collective-permute-start.5) | collective-permute-done | bytes 40992 | tf_op jit(solution)/shard_map/ppermute | solution.py:39
  159.7 0.1 collective-permute-done.4.refs_7_
  159.8 0.0 all-to-all-done.3
  159.8 1.4 backward_z.3
  161.2 2.3 %collective-permute-start.6 = (f32[32,8,256]{2,1,0:T(8,128)}, f32[32,8,256]{2,1,0:T(8,128)S(1)}, u32[]{:S(2)}, u32[]{:S(2)}) collective-permute-start(f32[32,8,256]{2,1,0:T(8,128)} %get-tuple-element.60), channel_id=1, source_target_pairs={{1,0},{2,1},{3,2},{4,3},{5,4},{6,5},{7,6},{0,7},{9,8},{10,9},{11,1... | collective-permute-start | bytes 786440 | tf_op jit(solution)/shard_map/ppermute | solution.py:29
  163.5 11.2 %interpolate.4.refs_12_ = f32[3,20480]{1,0:T(4,128)S(1)} custom-call(s32[512]{0:T(512)} %refs_0_.11, f32[3,32768]{1,0:T(4,128)S(1)} %copy-done, s32[2,32768]{1,0:T(2,128)S(1)} %copy-done.1, s32[256,128]{1,0:T(8,128)} %bitcast.13, f32[256,128]{1,0:T(8,128)} %bitcast.18, f32[8,32,256]{2,1,0:T(8,128)} %get-tuple-element.50.refs_5_, ...), custom_call_target="tpu_custom_call" | custom-call | tf_op jit(solution)/shard_map/interpolate/pallas_call | solution.py:371
  174.7 0.0 collective-permute-done.6.refs_9_
  174.7 5.3 %interpolate.5 = f32[3,32768]{1,0:T(4,128)} custom-call(s32[512]{0:T(512)} %refs_0_.11, f32[3,32768]{1,0:T(4,128)S(1)} %copy-done, s32[2,32768]{1,0:T(2,128)S(1)} %copy-done.1, s32[256,128]{1,0:T(8,128)} %bitcast.14, f32[256,128]{1,0:T(8,128)} %bitcast.19, f32[8,32,256]{2,1,0:T(8,128)} %get-tuple-element.50.refs_5_, ...), custom_call_target="tpu_custom_call" | custom-call | tf_op jit(solution)/shard_map/interpolate/pallas_call | solution.py:371
Async XLA Ops:
  0.6 13.1 %copy-start = (f32[3,32768]{1,0:T(4,128)S(1)}, f32[3,32768]{1,0:T(4,128)}, u32[]{:S(2)}) copy-start(f32[3,32768]{1,0:T(4,128)} %refs_1_.11) | copy-start | bytes 1179652
  0.6 13.1 %copy-start.1 = (s32[2,32768]{1,0:T(2,128)S(1)}, s32[2,32768]{1,0:T(2,128)}, u32[]{:S(2)}) copy-start(s32[2,32768]{1,0:T(2,128)} %refs_2_.9) | copy-start | bytes 786436
  0.6 20.7 %copy-start.2 = (bf16[256,256]{1,0:T(8,128)(2,1)S(1)}, bf16[256,256]{1,0:T(8,128)(2,1)}, u32[]{:S(2)}) copy-start(bf16[256,256]{1,0:T(8,128)(2,1)} %constant.34.refs_1_.refs_3_) | copy-start | bytes 393220
  0.7 20.7 %copy-start.3 = (bf16[256,256]{1,0:T(8,128)(2,1)S(1)}, bf16[256,256]{1,0:T(8,128)(2,1)}, u32[]{:S(2)}) copy-start(bf16[256,256]{1,0:T(8,128)(2,1)} %constant.31.refs_0_.refs_2_) | copy-start | bytes 393220
  9.6 11.7 %collective-permute-start = (f32[64,8,256]{2,1,0:T(8,128)}, f32[64,8,256]{2,1,0:T(8,128)S(1)}, u32[]{:S(2)}, u32[]{:S(2)}) collective-permute-start(f32[64,8,256]{2,1,0:T(8,128)} %get-tuple-element.39), channel_id=1, source_target_pairs={{7,0},{0,1},{1,2},{2,3},{3,4},{4,5},{5,6},{6,7},{15,8},{8,9},{9,10... | collective-permute-start | bytes 1572872 | tf_op jit(solution)/shard_map/ppermute | solution.py:29
  9.7 13.4 %collective-permute-start.1 = (f32[5,32,256]{2,1,0:T(8,128)}, f32[5,32,256]{2,1,0:T(8,128)S(1)}, u32[]{:S(2)}, u32[]{:S(2)}) collective-permute-start(f32[5,32,256]{2,1,0:T(8,128)} %get-tuple-element.40), channel_id=1, source_target_pairs={{24,0},{0,8},{8,16},{16,24},{25,1},{1,9},{9,17},{17,25},{26,2},{2,... | collective-permute-start | bytes 491528 | tf_op jit(solution)/shard_map/ppermute | solution.py:29
  11.2 11.8 %collective-permute-start.2 = (f32[5,8,256]{2,1,0:T(8,128)}, f32[5,8,256]{2,1,0:T(8,128)S(1)}, u32[]{:S(2)}, u32[]{:S(2)}) collective-permute-start(f32[5,8,256]{2,1,0:T(8,128)} %get-tuple-element.41), channel_id=1, source_target_pairs={{31,0},{24,1},{25,2},{26,3},{27,4},{28,5},{29,6},{30,7},{7,8},{0,9... | collective-permute-start | bytes 122888 | tf_op jit(solution)/shard_map/ppermute | solution.py:39
  23.0 29.1 %all-to-all-start.1 = ((f32[32,8,1024]{2,1,0:T(8,128)}), f32[32,8,1024]{2,1,0:T(8,128)S(1)}, u32[]{:S(2)}, u32[]{:S(2)}) async-start(f32[32,8,1024]{2,1,0:T(8,128)} %bitcast.4), calls=%async_computation.1 | async-start | bytes 2097152 | tf_op jit(solution)/shard_map/all_to_all | solution.py:700
  52.1 29.8 %all-to-all-start = ((f32[32,8,1024]{2,1,0:T(8,128)}), f32[32,8,1024]{2,1,0:T(8,128)S(1)}, u32[]{:S(2)}, u32[]{:S(2)}) async-start(f32[32,8,1024]{2,1,0:T(8,128)} %bitcast.3), calls=%async_computation | async-start | bytes 2097152 | tf_op jit(solution)/shard_map/all_to_all | solution.py:700
  93.7 29.8 %all-to-all-start.2 = ((f32[32,8,1024]{2,1,0:T(8,128)}), f32[32,8,1024]{2,1,0:T(8,128)S(1)}, u32[]{:S(2)}, u32[]{:S(2)}) async-start(f32[32,8,1024]{2,1,0:T(8,128)} %get-tuple-element.49), calls=%async_computation.2 | async-start | bytes 2097152 | tf_op jit(solution)/shard_map/all_to_all | solution.py:700
  102.8 25.3 %copy-start.4 = (bf16[256,256]{1,0:T(8,128)(2,1)S(1)}, bf16[256,256]{1,0:T(8,128)(2,1)}, u32[]{:S(2)}) copy-start(bf16[256,256]{1,0:T(8,128)(2,1)} %constant.48.low_ref) | copy-start | bytes 393220
  102.8 25.3 %copy-start.5 = (bf16[256,256]{1,0:T(8,128)(2,1)S(1)}, bf16[256,256]{1,0:T(8,128)(2,1)}, u32[]{:S(2)}) copy-start(bf16[256,256]{1,0:T(8,128)(2,1)} %constant.45.high_ref) | copy-start | bytes 393220
  123.5 36.3 %all-to-all-start.3 = ((f32[32,8,1152]{2,1,0:T(8,128)}), f32[32,8,1152]{2,1,0:T(8,128)S(1)}, u32[]{:S(2)}, u32[]{:S(2)}) async-start(f32[32,8,1152]{2,1,0:T(8,128)} %planes_last.1), calls=%async_computation.3 | async-start | bytes 2359296 | tf_op jit(solution)/shard_map/all_to_all | solution.py:700
  129.6 9.1 %collective-permute-start.3 = (f32[32,8,256]{2,1,0:T(8,128)}, f32[32,8,256]{2,1,0:T(8,128)S(1)}, u32[]{:S(2)}, u32[]{:S(2)}) collective-permute-start(f32[32,8,256]{2,1,0:T(8,128)} %get-tuple-element.54), channel_id=1, source_target_pairs={{1,0},{2,1},{3,2},{4,3},{5,4},{6,5},{7,6},{0,7},{9,8},{10,9},{11,1... | collective-permute-start | bytes 786440 | tf_op jit(solution)/shard_map/ppermute | solution.py:29
  131.7 28.2 %collective-permute-start.4 = (f32[5,32,256]{2,1,0:T(8,128)}, f32[5,32,256]{2,1,0:T(8,128)S(1)}, u32[]{:S(2)}, u32[]{:S(2)}) collective-permute-start(f32[5,32,256]{2,1,0:T(8,128)} %get-tuple-element.55), channel_id=1, source_target_pairs={{8,0},{16,8},{24,16},{0,24},{9,1},{17,9},{25,17},{1,25},{10,2},{18... | collective-permute-start | bytes 491528 | tf_op jit(solution)/shard_map/ppermute | solution.py:29
  132.2 27.5 %collective-permute-start.5 = (f32[5,8,256]{2,1,0:T(8,128)}, f32[5,8,256]{2,1,0:T(8,128)S(1)}, u32[]{:S(2)}, u32[]{:S(2)}) collective-permute-start(f32[5,8,256]{2,1,0:T(8,128)} %get-tuple-element.56), channel_id=1, source_target_pairs={{9,0},{10,1},{11,2},{12,3},{13,4},{14,5},{15,6},{8,7},{17,8},{18,9... | collective-permute-start | bytes 122888 | tf_op jit(solution)/shard_map/ppermute | solution.py:39
  161.2 13.5 %collective-permute-start.6 = (f32[32,8,256]{2,1,0:T(8,128)}, f32[32,8,256]{2,1,0:T(8,128)S(1)}, u32[]{:S(2)}, u32[]{:S(2)}) collective-permute-start(f32[32,8,256]{2,1,0:T(8,128)} %get-tuple-element.60), channel_id=1, source_target_pairs={{1,0},{2,1},{3,2},{4,3},{5,4},{6,5},{7,6},{0,7},{9,8},{10,9},{11,1... | collective-permute-start | bytes 786440 | tf_op jit(solution)/shard_map/ppermute | solution.py:29
